TPU v7x, 8 devices: a whole 2x2x1 slice. The times are simulated.
8 devices in a mesh: dep: 2 (over z, y), col: 2 (over x), row: 2 (over core).
Axes of the slice: x: 2, y: 2, z: 1, core: 2. Of those that a mesh axis runs over, the one named last changes fastest.
Arguments:
- a_mat: bfloat16 [3072, 3072], P('row', 'col')
- b_mat: bfloat16 [3072, 3072], P('row', 'col')
Outputs:
- output: float32 [3072, 3072], P('row', ('col', 'dep'))
All inputs are finite; a program needn't handle non-finite values.
Results may differ from a plain program's by a relative error of at most 0.001.
Values are sent between devices in bfloat16 or wider.
A program may use at most 1 GiB of HBM per device.

v0:
```python
import jax
import jax.numpy as jnp
from jax import lax
from jax.sharding import PartitionSpec as P


def solution(mesh):
    n_dep = mesh.shape['dep']
    n_row = mesh.shape['row']
    n_col = mesh.shape['col']

    def local_product(a_blk, b_blk):
        layer_idx = lax.axis_index('dep')
        rows_a, cols_a = a_blk.shape
        cols_b = b_blk.shape[1]
        unit_len = cols_a // (n_row * n_dep)
        a_part = a_blk.reshape(rows_a, n_row, n_dep, unit_len)
        a_part = lax.dynamic_index_in_dim(a_part, layer_idx, axis=2, keepdims=False)
        a_part = a_part.reshape(rows_a, n_row * unit_len)
        b_part = b_blk.reshape(n_col, n_dep, unit_len, cols_b)
        b_part = lax.dynamic_index_in_dim(b_part, layer_idx, axis=1, keepdims=False)
        b_part = b_part.reshape(n_col * unit_len, cols_b)
        a_panel = lax.all_gather(a_part, 'col', axis=1, tiled=True)
        b_panel = lax.all_gather(b_part, 'row', axis=0, tiled=True)
        part_sum = jnp.dot(a_panel, b_panel, preferred_element_type=jnp.float32)
        return lax.psum_scatter(part_sum, 'dep', scatter_dimension=1, tiled=True)

    return jax.shard_map(local_product, mesh=mesh, in_specs=(P('row', 'col'), P('row', 'col')), out_specs=P('row', ('col', 'dep')), check_vma=False)
```

profile of v0, /device:TPU:0, one launch (start us, length us, event | category | flops | bytes accessed | tf_op | source)
XLA Modules:
  0.0 215.3 jit_solution(2343817497505276499)
XLA Ops:
  6.5 0.0 all-gather.5.cloned.1.call-start
  6.5 3.2 %constant_dynamic-slice_fusion = bf16[2,1,384,1536]{3,2,1,0:T(8,128)(2,1)} fusion(bf16[2,2,384,1536]{3,2,1,0:T(8,128)(2,1)} %bitcast.9, s32[]{:T(128)S(6)} %select_n.6), kind=kLoop, calls=%fused_computation | loop fusion | bytes 4718596 | tf_op jit(solution)/shard_map/jit(dynamic_index_in_dim)/dynamic_slice | solution.py:21
  9.8 0.0 all-gather.5.cloned.1.call-update
  9.8 0.0 all-gather.3.cloned.1.call-start
  9.8 6.6 %copy.3 = bf16[1536,1536]{0,1:T(8,128)(2,1)} copy(bf16[1536,1536]{1,0:T(8,128)(2,1)} %param.2) | data formatting | bytes 9437184 | tf_op args[0]
  16.5 3.2 %constant_dynamic-slice_fusion.1 = bf16[1536,2,1,384]{0,3,2,1:T(8,128)(2,1)} fusion(bf16[1536,2,2,384]{0,3,2,1:T(8,128)(2,1)} %bitcast.6, s32[]{:T(128)S(6)} %select_n.6), kind=kLoop, calls=%fused_computation.1 | loop fusion | bytes 4718596 | tf_op jit(solution)/shard_map/jit(dynamic_index_in_dim)/dynamic_slice | solution.py:18
  19.7 0.0 all-gather.3.cloned.1.call-update
  19.7 0.0 reduce-scatter.2.cloned.1.call-start
  19.8 5.1 %all-gather.5.cloned.1.call-done = bf16[1536,1536]{1,0:T(8,128)(2,1)} async-done(((bf16[768,1536]{1,0:T(8,128)(2,1)}), bf16[1536,1536]{1,0:T(8,128)(2,1)}) %all-gather.5.cloned.1.call-update) | async-done | bytes 4718608 | tf_op jit(solution)/shard_map/all_gather | solution.py:24
  24.9 62.9 %all-gather.3.cloned.1.call-done = bf16[1536,1536]{0,1:T(8,128)(2,1)} async-done(((bf16[1536,768]{0,1:T(8,128)(2,1)}), bf16[1536,1536]{0,1:T(8,128)(2,1)}) %all-gather.3.cloned.1.call-update) | async-done | bytes 4718608 | tf_op jit(solution)/shard_map/all_gather | solution.py:23
  87.8 13.1 %fusion = f32[1536,1536]{1,0:T(8,128)} fusion(bf16[1536,1536]{0,1:T(8,128)(2,1)} %all-gather.3.cloned.1.call-done, bf16[1536,1536]{1,0:T(8,128)(2,1)} %all-gather.5.cloned.1.call-done), kind=kOutput, calls=%fused_computation.2 | convolution fusion | flops 7247757312 | bytes 18874368 | tf_op jit(solution)/shard_map/dot_general | solution.py:25
  100.9 0.0 reduce-scatter.2.cloned.1.call-update
  100.9 107.9 %reduce-scatter.2.cloned.1.call-done = f32[1536,768]{1,0:T(8,128)} async-done(((f32[1536,1536]{1,0:T(8,128)}), f32[1536,768]{1,0:T(8,128)}) %reduce-scatter.2.cloned.1.call-update) | async-done | bytes 4718608 | tf_op jit(solution)/shard_map/reduce_scatter | solution.py:26
Async XLA Ops:
  6.5 18.3 %all-gather.5.cloned.1.call-start = ((), (), s32[]{:S(2)}) async-start(), calls=%async_computation.2 | async-start | bytes 7077888 | tf_op jit(solution)/shard_map/all_gather | solution.py:24
  9.8 78.0 %all-gather.3.cloned.1.call-start = ((), (), s32[]{:S(2)}) async-start(), calls=%async_computation.1 | async-start | bytes 7077888 | tf_op jit(solution)/shard_map/all_gather | solution.py:23
  19.7 189.1 %reduce-scatter.2.cloned.1.call-start = ((), (), s32[]{:S(2)}) async-start(), calls=%async_computation.3 | async-start | bytes 14155776 | tf_op jit(solution)/shard_map/reduce_scatter | solution.py:26
Sparse Core Ops, SparseCore 0:
  9.9 14.8 all-gather.4
  26.4 61.3 all-gather.2
  101.0 107.7 reduce-scatter.1
where the time goes:
time: 216 us; the launch traced here: 215 us
  waiting for transfers between devices  176 us (81%)
  local copies, waits for them, and re-layouts  13.1 us (6%)
  matrix products  13.1 us (6%)
  between operations  13.1 us (6%)
    reduce_scatter x1, waiting for transfers between devices, local_product(): return lax.psum_scatter(part_sum, 'dep', scatter_dimension=1, tiled=True)  108 us
    all_gather x1, waiting for transfers between devices, local_product(): a_panel = lax.all_gather(a_part, 'col', axis=1, tiled=True)  62.9 us
    dot_general x1, matrix products, local_product(): part_sum = jnp.dot(a_panel, b_panel, preferred_element_type=jnp.float32)  13.1 us
    unnamed x1, local copies, waits for them, and re-layouts  6.62 us
    all_gather x1, waiting for transfers between devices, local_product(): b_panel = lax.all_gather(b_part, 'row', axis=0, tiled=True)  5.1 us
  transfers between devices with their start and end apart: 3, of which 3 were waited for; matrix products, arithmetic and copies ran while one was open for 5% of the time, Pallas kernels for 0%

commit v1 on v0

v1 whole, which is shorter than its diff:
```python
import functools

import jax
import jax.numpy as jnp
from jax import lax
from jax.experimental import pallas as pl
from jax.experimental.pallas import tpu as pltpu
from jax.sharding import PartitionSpec as P

MESH = pl.DeviceIdType.MESH
CHUNK = 32
LEAD = 2


def kernel(n_x, n_y, a_hbm, b_hbm, c_ref, a_loc, a_rem, b_full, a_sem, b_sem, x_send, x_recv, y_send, y_recv, d_send, d_recv):
    layer = lax.axis_index('dep')
    col = lax.axis_index('col')
    row = lax.axis_index('row')
    rows = a_loc.shape[0]
    width = b_full.shape[2]
    rest = rows - n_x * CHUNK

    def place(owner, idx):
        start = idx * CHUNK + owner * (rows - (2 * idx + 1) * CHUNK)
        return pl.ds(pl.multiple_of(start, CHUNK), CHUNK)

    def load_a(idx):
        sl = place(layer, idx)
        return pltpu.make_async_copy(a_hbm.at[sl], a_loc.at[sl], a_sem.at[idx])

    rest_sl = pl.ds(pl.multiple_of((1 - layer) * n_x * CHUNK, CHUNK), rest)
    load_rest = pltpu.make_async_copy(a_hbm.at[rest_sl], a_loc.at[rest_sl], a_sem.at[n_x])
    load_b = pltpu.make_async_copy(b_hbm.at[:, pl.ds(pl.multiple_of(layer * width, 128), width)], b_full.at[row], b_sem)

    def send_x(idx):
        sl = place(layer, idx)
        return pltpu.make_async_remote_copy(
            src_ref=a_loc.at[sl], dst_ref=a_rem.at[sl], send_sem=x_send.at[idx], recv_sem=x_recv.at[idx],
            device_id=(layer, 1 - col, row), device_id_type=MESH)

    def send_y(idx):
        sl = place(layer, idx)
        return pltpu.make_async_remote_copy(
            src_ref=a_rem.at[sl], dst_ref=a_rem.at[sl], send_sem=y_send.at[idx], recv_sem=y_recv.at[idx],
            device_id=(1 - layer, col, row), device_id_type=MESH)

    def recv_y(idx):
        sl = place(1 - layer, idx)
        return pltpu.make_async_remote_copy(
            src_ref=a_rem.at[sl], dst_ref=a_rem.at[sl], send_sem=y_send.at[idx], recv_sem=y_recv.at[idx],
            device_id=(1 - layer, col, row), device_id_type=MESH)

    def swap_b(half):
        return pltpu.make_async_remote_copy(
            src_ref=b_full.at[half], dst_ref=b_full.at[half], send_sem=d_send, recv_sem=d_recv,
            device_id=(layer, col, 1 - row), device_id_type=MESH)

    lax.fori_loop(0, n_x, lambda i, u: (load_a(i).start(), u)[1], 0)
    load_b.start()
    load_rest.start()

    barrier = pltpu.get_barrier_semaphore()
    for peer in ((layer, 1 - col, row), (1 - layer, col, row), (layer, col, 1 - row)):
        pl.semaphore_signal(barrier, inc=1, device_id=peer, device_id_type=MESH)
    pl.semaphore_wait(barrier, 3)

    def launch(i, u):
        load_a(i).wait()
        send_x(i).start()
        return u

    lax.fori_loop(0, n_x, launch, 0)
    load_b.wait()
    swap_b(row).start()
    load_rest.wait()
    swap_b(1 - row).wait_recv()

    def local(sl):
        c_ref[sl, :] = jnp.dot(a_loc[sl, :], b_full[col], preferred_element_type=jnp.float32)

    def remote(sl):
        c_ref[sl, :] += jnp.dot(a_rem[sl, :], b_full[1 - col], preferred_element_type=jnp.float32)

    def step(i, u):
        local(place(layer, i))
        send_x(i).wait_recv()

        @pl.when(i < n_y)
        def _():
            send_y(i).start()
            local(place(1 - layer, i))

        remote(place(layer, i))

        @pl.when(i >= LEAD)
        def _():
            recv_y(i - LEAD).wait_recv()
            remote(place(1 - layer, i - LEAD))

        return u

    lax.fori_loop(0, n_x, step, 0)

    lax.fori_loop(0, n_x, lambda i, u: (send_x(i).wait_send(), u)[1], 0)
    lax.fori_loop(0, n_y, lambda i, u: (send_y(i).wait_send(), u)[1], 0)
    swap_b(row).wait_send()


def solution(mesh):
    n_dep = mesh.shape['dep']

    def local_product(a_blk, b_blk):
        rows, depth = a_blk.shape
        width = b_blk.shape[1] // n_dep
        n_x = (rows // CHUNK + LEAD) // 2
        n_y = n_x - LEAD
        return pl.pallas_call(
            functools.partial(kernel, n_x, n_y),
            out_shape=pltpu.VMEM((rows, width), jnp.float32),
            in_specs=[pl.BlockSpec(memory_space=pltpu.HBM)] * 2,
            out_specs=pl.BlockSpec(memory_space=pltpu.VMEM),
            scratch_shapes=[
                pltpu.VMEM((rows, depth), jnp.bfloat16),
                pltpu.VMEM((rows, depth), jnp.bfloat16),
                pltpu.VMEM((2, depth, width), jnp.bfloat16),
                pltpu.SemaphoreType.DMA((n_x + 1,)),
                pltpu.SemaphoreType.DMA,
                pltpu.SemaphoreType.DMA((n_x,)),
                pltpu.SemaphoreType.DMA((n_x,)),
                pltpu.SemaphoreType.DMA((n_y,)),
                pltpu.SemaphoreType.DMA((n_y,)),
                pltpu.SemaphoreType.DMA,
                pltpu.SemaphoreType.DMA,
            ],
            compiler_params=pltpu.CompilerParams(collective_id=0, has_side_effects=True, vmem_limit_bytes=40 * 1024 * 1024),
            name='gather_dot',
        )(pltpu.with_memory_space_constraint(a_blk, pltpu.HBM), pltpu.with_memory_space_constraint(b_blk, pltpu.HBM))

    return jax.shard_map(local_product, mesh=mesh, in_specs=(P('row', 'col'), P('row', 'col')), out_specs=P('row', ('col', 'dep')), check_vma=False)
```

time: 216 us -> 64.5 us (0.30)
  waiting for transfers between devices: 176 us -> 0 us
  Pallas kernels: 0 us -> 62.2 us
  matrix products: 13.1 us -> 0 us
  between operations: 13.1 us -> 0.01 us
  local copies, waits for them, and re-layouts: 13.1 us -> 2.19 us
    reduce_scatter x1 -> x0, waiting for transfers between devices: 108 us -> none  [local_product(): return lax.psum_scatter(part_sum, 'dep', scatter_dimension=1, tiled=True)]
    all_gather x2 -> x0, waiting for transfers between devices: 68 us -> none  [the longest x1 62.9 us: local_product(): a_panel = lax.all_gather(a_part, 'col', axis=1, tiled=True)]
    pallas_call x0 -> x1, Pallas kernels: none -> 62.2 us  [local_product(): pl.pallas_call(functools.partial(kernel, n_x, n_y), out_shape=pltpu.VMEM(...]
    dot_general x1 -> x0, matrix products: 13.1 us -> none  [local_product(): part_sum = jnp.dot(a_panel, b_panel, preferred_element_type=jnp.float32)]
    dynamic_slice x2 -> x0, local copies, waits for them, and re-layouts: 6.45 us -> none  [the longest x1 3.23 us: local_product(): b_part = lax.dynamic_index_in_dim(b_part, layer_idx, axis=1, keepdims=False)]
    unnamed x1, local copies, waits for them, and re-layouts: 6.62 us -> 2.19 us
  transfers between devices with their start and end apart: 3 -> 0, of which waited for: 3 -> 0; matrix products, arithmetic and copies ran while one was open for 5% -> 0% of each run, Pallas kernels for 0% -> 0%
where the time goes in v1:
time: 64.5 us; the launch traced here: 64.4 us
  Pallas kernels  62.2 us (96%)
  local copies, waits for them, and re-layouts  2.19 us (3%)
    pallas_call x1, Pallas kernels, local_product(): pl.pallas_call(functools.partial(kernel, n_x, n_y), out_shape=pltpu.VMEM(...  62.2 us
    unnamed x1, local copies, waits for them, and re-layouts  2.19 us

profile of v1, /device:TPU:0, one launch (start us, length us, event | category | flops | bytes accessed | tf_op | source)
XLA Modules:
  0.0 64.4 jit_solution(9397208596251730117)
XLA Ops:
  0.0 62.2 %gather_dot.1 = f32[1536,768]{1,0:T(8,128)S(1)} custom-call(bf16[1536,1536]{1,0:T(8,128)(2,1)} %a_hbm.1, bf16[1536,1536]{1,0:T(8,128)(2,1)} %b_hbm.1), custom_call_target="tpu_custom_call" | custom-call | tf_op jit(solution)/shard_map/gather_dot/pallas_call | solution.py:117
  62.2 2.2 %copy.4 = f32[1536,768]{1,0:T(8,128)} copy(f32[1536,768]{1,0:T(8,128)S(1)} %gather_dot.1) | data formatting | bytes 9437184

commit v2 on v1

v2 whole, which is shorter than its diff:
```python
import functools

import jax
import jax.numpy as jnp
from jax import lax
from jax.experimental import pallas as pl
from jax.experimental.pallas import tpu as pltpu
from jax.sharding import PartitionSpec as P

MESH = pl.DeviceIdType.MESH
CHUNK = 16
GROUP = 4
LEAD = 4
HEAD = 4
NEXT = 16
BLOCK = 256
WARM = 6


def kernel(n_x, n_y, a_hbm, b_hbm, c_ref, a_loc, a_rem, b_full, a_sem, b_sem, x_send, x_recv, y_send, y_recv, d_send, d_recv, y_ready, d_ready):
    layer = lax.axis_index('dep')
    col = lax.axis_index('col')
    row = lax.axis_index('row')
    rows = a_loc.shape[0]
    width = b_full.shape[2]
    x_peer = (layer, 1 - col, row)
    y_peer = (1 - layer, col, row)
    d_peer = (layer, col, 1 - row)

    barrier = pltpu.get_barrier_semaphore()
    pl.semaphore_signal(barrier, inc=1, device_id=x_peer, device_id_type=MESH)

    @pl.when(layer == 0)
    def _():
        pl.semaphore_signal(barrier, inc=1, device_id=y_peer, device_id_type=MESH)

    @pl.when(row == 1)
    def _():
        pl.semaphore_signal(barrier, inc=1, device_id=d_peer, device_id_type=MESH)

    def place(owner, idx, count):
        start = idx * CHUNK + owner * (rows - (2 * idx + count) * CHUNK)
        return pl.ds(pl.multiple_of(start, CHUNK), count * CHUNK)

    def load_a(idx, count, sem):
        sl = place(layer, idx, count)
        return pltpu.make_async_copy(a_hbm.at[sl], a_loc.at[sl], a_sem.at[sem])

    loads = [load_a(i, 1, i) for i in range(HEAD)]
    loads.append(load_a(HEAD, NEXT - HEAD, HEAD))
    loads.append(load_a(NEXT, rows // CHUNK - NEXT, HEAD + 1))
    load_b = pltpu.make_async_copy(b_hbm.at[:, pl.ds(pl.multiple_of(layer * width, 128), width)], b_full.at[row], b_sem)

    def send_x(idx):
        sl = place(layer, idx, 1)
        return pltpu.make_async_remote_copy(
            src_ref=a_loc.at[sl], dst_ref=a_rem.at[sl], send_sem=x_send.at[idx], recv_sem=x_recv.at[idx],
            device_id=x_peer, device_id_type=MESH)

    def copy_y(owner, idx):
        sl = place(owner, idx, 1)
        return pltpu.make_async_remote_copy(
            src_ref=a_rem.at[sl], dst_ref=a_rem.at[sl], send_sem=y_send.at[idx], recv_sem=y_recv.at[idx],
            device_id=y_peer, device_id_type=MESH)

    def swap_b(half):
        return pltpu.make_async_remote_copy(
            src_ref=b_full.at[half], dst_ref=b_full.at[half], send_sem=d_send, recv_sem=d_recv,
            device_id=d_peer, device_id_type=MESH)

    for copy in loads[:HEAD + 1]:
        copy.start()
    load_b.start()
    loads[HEAD + 1].start()

    pl.semaphore_wait(barrier, 2 + layer - row)

    for i in range(HEAD):
        loads[i].wait()
        send_x(i).start()

    @pl.when(layer == 1)
    def _():
        pl.semaphore_signal(y_ready, inc=1, device_id=y_peer, device_id_type=MESH)

    @pl.when(row == 0)
    def _():
        pl.semaphore_signal(d_ready, inc=1, device_id=d_peer, device_id_type=MESH)

    def launch(i, u):
        send_x(i).start()
        return u

    loads[HEAD].wait()
    lax.fori_loop(HEAD, NEXT, launch, 0)
    load_b.wait()

    @pl.when(row == 1)
    def _():
        pl.semaphore_wait(d_ready, 1)

    swap_b(row).start()
    loads[HEAD + 1].wait()
    lax.fori_loop(NEXT, n_x, launch, 0)

    @pl.when(layer == 0)
    def _():
        pl.semaphore_wait(y_ready, 1)

    def remote(sl):
        c_ref[sl, :] += jnp.dot(a_rem[sl, :], b_full[1 - col], preferred_element_type=jnp.float32)

    n_local = rows // BLOCK
    join = WARM + n_local
    g_x = n_x // GROUP
    g_y = n_y // GROUP

    def step(i, u):
        @pl.when(i < n_x)
        def _():
            send_x(i).wait_recv()

        @pl.when(i < n_y)
        def _():
            copy_y(layer, i).start()

        @pl.when(i == WARM)
        def _():
            swap_b(1 - row).wait_recv()

        @pl.when((i >= WARM) & (i < join))
        def _():
            sl = pl.ds(pl.multiple_of((i - WARM) * BLOCK, BLOCK), BLOCK)
            c_ref[sl, :] = jnp.dot(a_loc[sl, :], b_full[col], preferred_element_type=jnp.float32)

        first_y = join + GROUP
        x_turn = jnp.where(i < first_y, i - join, jnp.where(i % GROUP == GROUP - 1, i // GROUP, -1))
        x_turn = jnp.where((i < first_y) | (i >= first_y + GROUP - 1), x_turn, -1)
        y_turn = jnp.where(i < first_y + GROUP - 1, i - first_y, jnp.where(i % GROUP == 0, i // GROUP - 2, -1))
        is_x = (x_turn >= 0) & (x_turn < g_x)
        is_y = (y_turn >= 0) & (y_turn < g_y)

        @pl.when(is_y)
        def _():
            for k in range(GROUP):
                copy_y(1 - layer, y_turn * GROUP + k).wait_recv()

        @pl.when(is_x | is_y)
        def _():
            owner = jnp.where(is_x, layer, 1 - layer)
            remote(place(owner, jnp.where(is_x, x_turn, y_turn) * GROUP, GROUP))

        return u

    lax.fori_loop(0, max(n_x, (g_y + 1) * GROUP + 1), step, 0)

    for k in range(g_y * GROUP, n_y):
        copy_y(1 - layer, k).wait_recv()
    if n_x % GROUP:
        remote(place(layer, g_x * GROUP, GROUP))

    lax.fori_loop(0, n_x, lambda i, u: (send_x(i).wait_send(), u)[1], 0)
    lax.fori_loop(0, n_y, lambda i, u: (copy_y(layer, i).wait_send(), u)[1], 0)
    swap_b(row).wait_send()


def solution(mesh):
    n_dep = mesh.shape['dep']

    def local_product(a_blk, b_blk):
        rows, depth = a_blk.shape
        width = b_blk.shape[1] // n_dep
        n_x = (rows // CHUNK + LEAD) // 2
        n_y = n_x - LEAD
        return pl.pallas_call(
            functools.partial(kernel, n_x, n_y),
            out_shape=pltpu.VMEM((rows, width), jnp.float32),
            in_specs=[pl.BlockSpec(memory_space=pltpu.HBM)] * 2,
            out_specs=pl.BlockSpec(memory_space=pltpu.VMEM),
            scratch_shapes=[
                pltpu.VMEM((rows, depth), jnp.bfloat16),
                pltpu.VMEM((rows, depth), jnp.bfloat16),
                pltpu.VMEM((2, depth, width), jnp.bfloat16),
                pltpu.SemaphoreType.DMA((HEAD + 2,)),
                pltpu.SemaphoreType.DMA,
                pltpu.SemaphoreType.DMA((n_x,)),
                pltpu.SemaphoreType.DMA((n_x,)),
                pltpu.SemaphoreType.DMA((n_y,)),
                pltpu.SemaphoreType.DMA((n_y,)),
                pltpu.SemaphoreType.DMA,
                pltpu.SemaphoreType.DMA,
                pltpu.SemaphoreType.REGULAR,
                pltpu.SemaphoreType.REGULAR,
            ],
            compiler_params=pltpu.CompilerParams(collective_id=0, has_side_effects=True, vmem_limit_bytes=40 * 1024 * 1024),
            name='gather_dot',
        )(pltpu.with_memory_space_constraint(a_blk, pltpu.HBM), pltpu.with_memory_space_constraint(b_blk, pltpu.HBM))

    return jax.shard_map(local_product, mesh=mesh, in_specs=(P('row', 'col'), P('row', 'col')), out_specs=P('row', ('col', 'dep')), check_vma=False)
```

time: 64.5 us -> 63 us (0.977)
  Pallas kernels: 62.2 us -> 60.7 us
    pallas_call x1, Pallas kernels: 62.2 us -> 60.7 us  [local_product(): pl.pallas_call(functools.partial(kernel, n_x, n_y), out_shape=pltpu.VMEM(...]
where the time goes in v2:
time: 63 us; the launch traced here: 62.9 us
  Pallas kernels  60.7 us (96%)
  local copies, waits for them, and re-layouts  2.19 us (3%)
    pallas_call x1, Pallas kernels, local_product(): pl.pallas_call(functools.partial(kernel, n_x, n_y), out_shape=pltpu.VMEM(...  60.7 us
    unnamed x1, local copies, waits for them, and re-layouts  2.19 us

profile of v2, /device:TPU:0, one launch (start us, length us, event | category | flops | bytes accessed | tf_op | source)
XLA Modules:
  0.0 62.9 jit_solution(3560613492468346662)
XLA Ops:
  0.0 60.7 %gather_dot.1 = f32[1536,768]{1,0:T(8,128)S(1)} custom-call(bf16[1536,1536]{1,0:T(8,128)(2,1)} %a_hbm.1, bf16[1536,1536]{1,0:T(8,128)(2,1)} %b_hbm.1), custom_call_target="tpu_custom_call" | custom-call | tf_op jit(solution)/shard_map/gather_dot/pallas_call | solution.py:175
  60.7 2.2 %copy.4 = f32[1536,768]{1,0:T(8,128)} copy(f32[1536,768]{1,0:T(8,128)S(1)} %gather_dot.1) | data formatting | bytes 9437184

commit v3 on v2

--- a/solution.py
+++ b/solution.py
@@ -8,13 +8,14 @@
 from jax.sharding import PartitionSpec as P
 
 MESH = pl.DeviceIdType.MESH
-CHUNK = 16
-GROUP = 4
-LEAD = 4
-HEAD = 4
-NEXT = 16
+CHUNK = 32
+GROUP = 64 // CHUNK
+LEAD = 64 // CHUNK
+LAG = 80 // CHUNK
+HEAD = 64 // CHUNK
+NEXT = 256 // CHUNK
 BLOCK = 256
-WARM = 6
+WARM = 96 // CHUNK
 
 
 def kernel(n_x, n_y, a_hbm, b_hbm, c_ref, a_loc, a_rem, b_full, a_sem, b_sem, x_send, x_recv, y_send, y_recv, d_send, d_recv, y_ready, d_ready):
@@ -110,12 +111,13 @@
     def remote(sl):
         c_ref[sl, :] += jnp.dot(a_rem[sl, :], b_full[1 - col], preferred_element_type=jnp.float32)
 
-    n_local = rows // BLOCK
-    join = WARM + n_local
+    join = WARM + rows // BLOCK
     g_x = n_x // GROUP
     g_y = n_y // GROUP
 
-    def step(i, u):
+    def step(i, done):
+        x_done, y_done = done
+
         @pl.when(i < n_x)
         def _():
             send_x(i).wait_recv()
@@ -133,26 +135,22 @@
             sl = pl.ds(pl.multiple_of((i - WARM) * BLOCK, BLOCK), BLOCK)
             c_ref[sl, :] = jnp.dot(a_loc[sl, :], b_full[col], preferred_element_type=jnp.float32)
 
-        first_y = join + GROUP
-        x_turn = jnp.where(i < first_y, i - join, jnp.where(i % GROUP == GROUP - 1, i // GROUP, -1))
-        x_turn = jnp.where((i < first_y) | (i >= first_y + GROUP - 1), x_turn, -1)
-        y_turn = jnp.where(i < first_y + GROUP - 1, i - first_y, jnp.where(i % GROUP == 0, i // GROUP - 2, -1))
-        is_x = (x_turn >= 0) & (x_turn < g_x)
-        is_y = (y_turn >= 0) & (y_turn < g_y)
+        is_x = (i >= join) & (x_done < g_x) & ((x_done + 1) * GROUP <= i + 1)
+        is_y = (i >= join) & (y_done < g_y) & ((y_done + 1) * GROUP + LAG <= i + 1)
+
+        @pl.when(is_x)
+        def _():
+            remote(place(layer, x_done * GROUP, GROUP))
 
         @pl.when(is_y)
         def _():
             for k in range(GROUP):
-                copy_y(1 - layer, y_turn * GROUP + k).wait_recv()
+                copy_y(1 - layer, y_done * GROUP + k).wait_recv()
+            remote(place(1 - layer, y_done * GROUP, GROUP))
 
-        @pl.when(is_x | is_y)
-        def _():
-            owner = jnp.where(is_x, layer, 1 - layer)
-            remote(place(owner, jnp.where(is_x, x_turn, y_turn) * GROUP, GROUP))
+        return x_done + is_x.astype(jnp.int32), y_done + is_y.astype(jnp.int32)
 
-        return u
-
-    lax.fori_loop(0, max(n_x, (g_y + 1) * GROUP + 1), step, 0)
+    lax.fori_loop(0, max(n_x, g_y * GROUP + LAG), step, (0, 0))
 
     for k in range(g_y * GROUP, n_y):
         copy_y(1 - layer, k).wait_recv()

time: 63 us -> 62.4 us (level)
  no operation moved by 1% of the time
where the time goes in v3:
time: 62.4 us; the launch traced here: 62.3 us
  Pallas kernels  60.1 us (96%)
  local copies, waits for them, and re-layouts  2.19 us (4%)
    pallas_call x1, Pallas kernels, local_product(): pl.pallas_call(functools.partial(kernel, n_x, n_y), out_shape=pltpu.VMEM(...  60.1 us
    unnamed x1, local copies, waits for them, and re-layouts  2.19 us

profile of v3, /device:TPU:0, one launch (start us, length us, event | category | flops | bytes accessed | tf_op | source)
XLA Modules:
  0.0 62.3 jit_solution(13821947060032113733)
XLA Ops:
  0.0 60.1 %gather_dot.1 = f32[1536,768]{1,0:T(8,128)S(1)} custom-call(bf16[1536,1536]{1,0:T(8,128)(2,1)} %a_hbm.1, bf16[1536,1536]{1,0:T(8,128)(2,1)} %b_hbm.1), custom_call_target="tpu_custom_call" | custom-call | tf_op jit(solution)/shard_map/gather_dot/pallas_call | solution.py:173
  60.1 2.2 %copy.4 = f32[1536,768]{1,0:T(8,128)} copy(f32[1536,768]{1,0:T(8,128)S(1)} %gather_dot.1) | data formatting | bytes 9437184

commit v4 on v3

--- a/solution.py
+++ b/solution.py
@@ -1,5 +1,3 @@
-import functools
-
 import jax
 import jax.numpy as jnp
 from jax import lax
@@ -7,10 +5,10 @@
 from jax.experimental.pallas import tpu as pltpu
 from jax.sharding import PartitionSpec as P
 
+TAKE = (((26, 26), (24, 24)), ((26, 26), (24, 24)))
 MESH = pl.DeviceIdType.MESH
 CHUNK = 32
 GROUP = 64 // CHUNK
-LEAD = 64 // CHUNK
 LAG = 80 // CHUNK
 HEAD = 64 // CHUNK
 NEXT = 256 // CHUNK
@@ -18,12 +16,26 @@
 WARM = 96 // CHUNK
 
 
-def kernel(n_x, n_y, a_hbm, b_hbm, c_ref, a_loc, a_rem, b_full, a_sem, b_sem, x_send, x_recv, y_send, y_recv, d_send, d_recv, y_ready, d_ready):
+def taken(layer, col, row):
+    total = 0
+    for l in range(2):
+        for j in range(2):
+            for i in range(2):
+                total += TAKE[l][j][i] * (l * layer + (1 - l) * (1 - layer)) * (j * col + (1 - j) * (1 - col)) * (i * row + (1 - i) * (1 - row))
+    return total
+
+
+def kernel(a_hbm, b_hbm, c_ref, a_loc, a_rem, b_full, a_sem, b_sem, x_send, x_recv, y_send, y_recv, d_send, d_recv, y_ready, d_ready):
     layer = lax.axis_index('dep')
     col = lax.axis_index('col')
     row = lax.axis_index('row')
     rows = a_loc.shape[0]
     width = b_full.shape[2]
+    chunks = rows // CHUNK
+    n_x = taken(layer, col, row)
+    n_y = chunks - n_x
+    n_out = taken(layer, 1 - col, row)
+    n_pass = chunks - taken(1 - layer, col, row)
     x_peer = (layer, 1 - col, row)
     y_peer = (1 - layer, col, row)
     d_peer = (layer, col, 1 - row)
@@ -102,7 +114,7 @@
 
     swap_b(row).start()
     loads[HEAD + 1].wait()
-    lax.fori_loop(NEXT, n_x, launch, 0)
+    lax.fori_loop(NEXT, n_out, launch, 0)
 
     @pl.when(layer == 0)
     def _():
@@ -122,7 +134,7 @@
         def _():
             send_x(i).wait_recv()
 
-        @pl.when(i < n_y)
+        @pl.when(i < n_pass)
         def _():
             copy_y(layer, i).start()
 
@@ -150,15 +162,16 @@
 
         return x_done + is_x.astype(jnp.int32), y_done + is_y.astype(jnp.int32)
 
-    lax.fori_loop(0, max(n_x, g_y * GROUP + LAG), step, (0, 0))
-
-    for k in range(g_y * GROUP, n_y):
-        copy_y(1 - layer, k).wait_recv()
-    if n_x % GROUP:
+    lax.fori_loop(0, jnp.maximum(n_x, g_y * GROUP + LAG), step, (0, 0))
+
+    lax.fori_loop(g_y * GROUP, n_y, lambda i, u: (copy_y(1 - layer, i).wait_recv(), u)[1], 0)
+
+    @pl.when(g_x + g_y < chunks // GROUP)
+    def _():
         remote(place(layer, g_x * GROUP, GROUP))
 
-    lax.fori_loop(0, n_x, lambda i, u: (send_x(i).wait_send(), u)[1], 0)
-    lax.fori_loop(0, n_y, lambda i, u: (copy_y(layer, i).wait_send(), u)[1], 0)
+    lax.fori_loop(0, n_out, lambda i, u: (send_x(i).wait_send(), u)[1], 0)
+    lax.fori_loop(0, n_pass, lambda i, u: (copy_y(layer, i).wait_send(), u)[1], 0)
     swap_b(row).wait_send()
 
 
@@ -168,10 +181,9 @@
     def local_product(a_blk, b_blk):
         rows, depth = a_blk.shape
         width = b_blk.shape[1] // n_dep
-        n_x = (rows // CHUNK + LEAD) // 2
-        n_y = n_x - LEAD
+        chunks = rows // CHUNK
         return pl.pallas_call(
-            functools.partial(kernel, n_x, n_y),
+            kernel,
             out_shape=pltpu.VMEM((rows, width), jnp.float32),
             in_specs=[pl.BlockSpec(memory_space=pltpu.HBM)] * 2,
             out_specs=pl.BlockSpec(memory_space=pltpu.VMEM),
@@ -181,10 +193,10 @@
                 pltpu.VMEM((2, depth, width), jnp.bfloat16),
                 pltpu.SemaphoreType.DMA((HEAD + 2,)),
                 pltpu.SemaphoreType.DMA,
-                pltpu.SemaphoreType.DMA((n_x,)),
-                pltpu.SemaphoreType.DMA((n_x,)),
-                pltpu.SemaphoreType.DMA((n_y,)),
-                pltpu.SemaphoreType.DMA((n_y,)),
+                pltpu.SemaphoreType.DMA((chunks,)),
+                pltpu.SemaphoreType.DMA((chunks,)),
+                pltpu.SemaphoreType.DMA((chunks,)),
+                pltpu.SemaphoreType.DMA((chunks,)),
                 pltpu.SemaphoreType.DMA,
                 pltpu.SemaphoreType.DMA,
                 pltpu.SemaphoreType.REGULAR,

time: 62.4 us -> 64.6 us (1.035)
  Pallas kernels: 60.1 us -> 62.3 us
    pallas_call x1, Pallas kernels: 60.1 us -> 62.3 us  [local_product(): pl.pallas_call(kernel, out_shape=pltpu.VMEM((rows, width), jnp.float32),...]
where the time goes in v4:
time: 64.6 us; the launch traced here: 64.5 us
  Pallas kernels  62.3 us (96%)
  local copies, waits for them, and re-layouts  2.19 us (3%)
    pallas_call x1, Pallas kernels, local_product(): pl.pallas_call(kernel, out_shape=pltpu.VMEM((rows, width), jnp.float32),...  62.3 us
    unnamed x1, local copies, waits for them, and re-layouts  2.19 us

profile of v4, /device:TPU:0, one launch (start us, length us, event | category | flops | bytes accessed | tf_op | source)
XLA Modules:
  0.0 64.5 jit_solution(18369825902436779260)
XLA Ops:
  0.0 62.3 %gather_dot.1 = f32[1536,768]{1,0:T(8,128)S(1)} custom-call(bf16[1536,1536]{1,0:T(8,128)(2,1)} %a_hbm.1, bf16[1536,1536]{1,0:T(8,128)(2,1)} %b_hbm.1), custom_call_target="tpu_custom_call" | custom-call | tf_op jit(solution)/shard_map/gather_dot/pallas_call | solution.py:185
  62.3 2.2 %copy.4 = f32[1536,768]{1,0:T(8,128)} copy(f32[1536,768]{1,0:T(8,128)S(1)} %gather_dot.1) | data formatting | bytes 9437184

commit v5 on v4

--- a/solution.py
+++ b/solution.py
@@ -5,7 +5,7 @@
 from jax.experimental.pallas import tpu as pltpu
 from jax.sharding import PartitionSpec as P
 
-TAKE = (((26, 26), (24, 24)), ((26, 26), (24, 24)))
+TAKE = (((24, 25), (24, 25)), ((24, 25), (24, 25)))
 MESH = pl.DeviceIdType.MESH
 CHUNK = 32
 GROUP = 64 // CHUNK
@@ -13,6 +13,7 @@
 HEAD = 64 // CHUNK
 NEXT = 256 // CHUNK
 BLOCK = 256
+LEFT = 5
 WARM = 96 // CHUNK
 
 
@@ -25,7 +26,7 @@
     return total
 
 
-def kernel(a_hbm, b_hbm, c_ref, a_loc, a_rem, b_full, a_sem, b_sem, x_send, x_recv, y_send, y_recv, d_send, d_recv, y_ready, d_ready):
+def kernel(a_hbm, b_hbm, c_ref, a_loc, a_rem, b_full, a_sem, b_sem, x_send, x_recv, y_send, y_recv, d_send, d_recv, y_ready, d_ready, go):
     layer = lax.axis_index('dep')
     col = lax.axis_index('col')
     row = lax.axis_index('row')
@@ -90,7 +91,10 @@
 
     for i in range(HEAD):
         loads[i].wait()
-        send_x(i).start()
+
+        @pl.when(row == 0)
+        def _():
+            send_x(i).start()
 
     @pl.when(layer == 1)
     def _():
@@ -105,7 +109,11 @@
         return u
 
     loads[HEAD].wait()
-    lax.fori_loop(HEAD, NEXT, launch, 0)
+
+    @pl.when(row == 0)
+    def _():
+        lax.fori_loop(HEAD, NEXT, launch, 0)
+
     load_b.wait()
 
     @pl.when(row == 1)
@@ -114,7 +122,15 @@
 
     swap_b(row).start()
     loads[HEAD + 1].wait()
-    lax.fori_loop(NEXT, n_out, launch, 0)
+
+    @pl.when(row == 0)
+    def _():
+        lax.fori_loop(NEXT, n_out, launch, 0)
+
+    @pl.when(row == 1)
+    def _():
+        pl.semaphore_wait(go, 1)
+        lax.fori_loop(0, n_out, launch, 0)
 
     @pl.when(layer == 0)
     def _():
@@ -137,6 +153,10 @@
         @pl.when(i < n_pass)
         def _():
             copy_y(layer, i).start()
+
+        @pl.when((i == n_x - LEFT) & (row == 0))
+        def _():
+            pl.semaphore_signal(go, inc=1, device_id=d_peer, device_id_type=MESH)
 
         @pl.when(i == WARM)
         def _():
@@ -201,6 +221,7 @@
                 pltpu.SemaphoreType.DMA,
                 pltpu.SemaphoreType.REGULAR,
                 pltpu.SemaphoreType.REGULAR,
+                pltpu.SemaphoreType.REGULAR,
             ],
             compiler_params=pltpu.CompilerParams(collective_id=0, has_side_effects=True, vmem_limit_bytes=40 * 1024 * 1024),
             name='gather_dot',

time: 64.6 us -> 65.7 us (1.017)
  the two profiles are of different devices: /device:TPU:0 before, /device:TPU:1 now
where the time goes in v5:
time: 65.7 us; the launch traced here: 65.6 us
  Pallas kernels  63.4 us (96%)
  local copies, waits for them, and re-layouts  2.19 us (3%)
    pallas_call x1, Pallas kernels, local_product(): pl.pallas_call(kernel, out_shape=pltpu.VMEM((rows, width), jnp.float32),...  63.4 us
    unnamed x1, local copies, waits for them, and re-layouts  2.19 us

profile of v5, /device:TPU:1, one launch (start us, length us, event | category | flops | bytes accessed | tf_op | source)
XLA Modules:
  0.0 65.6 jit_solution(6649787794119025479)
XLA Ops:
  0.0 63.4 %gather_dot.1 = f32[1536,768]{1,0:T(8,128)S(1)} custom-call(bf16[1536,1536]{1,0:T(8,128)(2,1)} %a_hbm.1, bf16[1536,1536]{1,0:T(8,128)(2,1)} %b_hbm.1), custom_call_target="tpu_custom_call" | custom-call | tf_op jit(solution)/shard_map/gather_dot/pallas_call | solution.py:205
  63.4 2.2 %copy.4 = f32[1536,768]{1,0:T(8,128)} copy(f32[1536,768]{1,0:T(8,128)S(1)} %gather_dot.1) | data formatting | bytes 9437184

commit v6 on v4

--- a/solution.py
+++ b/solution.py
@@ -5,7 +5,7 @@
 from jax.experimental.pallas import tpu as pltpu
 from jax.sharding import PartitionSpec as P
 
-TAKE = (((26, 26), (24, 24)), ((26, 26), (24, 24)))
+TAKE = (((25, 25), (25, 25)), ((25, 25), (25, 25)))
 MESH = pl.DeviceIdType.MESH
 CHUNK = 32
 GROUP = 64 // CHUNK
@@ -13,6 +13,7 @@
 HEAD = 64 // CHUNK
 NEXT = 256 // CHUNK
 BLOCK = 256
+HOLD = 12
 WARM = 96 // CHUNK
 
 
@@ -114,7 +115,8 @@
 
     swap_b(row).start()
     loads[HEAD + 1].wait()
-    lax.fori_loop(NEXT, n_out, launch, 0)
+    first_out = jnp.where(row == 0, n_out, HOLD)
+    lax.fori_loop(NEXT, first_out, launch, 0)
 
     @pl.when(layer == 0)
     def _():
@@ -137,6 +139,10 @@
         @pl.when(i < n_pass)
         def _():
             copy_y(layer, i).start()
+
+        @pl.when(i == HOLD - 1)
+        def _():
+            lax.fori_loop(first_out, n_out, launch, 0)
 
         @pl.when(i == WARM)
         def _():

time: 64.6 us -> 62.6 us (0.969)
  Pallas kernels: 62.3 us -> 60.3 us
    pallas_call x1, Pallas kernels: 62.3 us -> 60.3 us  [local_product(): pl.pallas_call(kernel, out_shape=pltpu.VMEM((rows, width), jnp.float32),...]
where the time goes in v6:
time: 62.6 us; the launch traced here: 62.5 us
  Pallas kernels  60.3 us (96%)
  local copies, waits for them, and re-layouts  2.19 us (3%)
    pallas_call x1, Pallas kernels, local_product(): pl.pallas_call(kernel, out_shape=pltpu.VMEM((rows, width), jnp.float32),...  60.3 us
    unnamed x1, local copies, waits for them, and re-layouts  2.19 us

profile of v6, /device:TPU:0, one launch (start us, length us, event | category | flops | bytes accessed | tf_op | source)
XLA Modules:
  0.0 62.5 jit_solution(14926719082410112489)
XLA Ops:
  0.0 60.3 %gather_dot.1 = f32[1536,768]{1,0:T(8,128)S(1)} custom-call(bf16[1536,1536]{1,0:T(8,128)(2,1)} %a_hbm.1, bf16[1536,1536]{1,0:T(8,128)(2,1)} %b_hbm.1), custom_call_target="tpu_custom_call" | custom-call | tf_op jit(solution)/shard_map/gather_dot/pallas_call | solution.py:191
  60.3 2.2 %copy.4 = f32[1536,768]{1,0:T(8,128)} copy(f32[1536,768]{1,0:T(8,128)S(1)} %gather_dot.1) | data formatting | bytes 9437184

commit v7 on v3

v7 whole, which is shorter than its diff:
```python
import jax
import jax.numpy as jnp
from jax import lax
from jax.experimental import pallas as pl
from jax.experimental.pallas import tpu as pltpu
from jax.sharding import PartitionSpec as P

MESH = pl.DeviceIdType.MESH
FIRST = 16
CHUNK = 32
GROUP = 2
LAG = 2
HEAD = 3
NEXT = 9
BLOCK = 256
WARM = 3
TAKE = (26, 25)


def kernel(a_hbm, b_hbm, c_ref, a_loc, a_rem, b_full, stage, a_sem, b_sem, x_send, x_recv, y_send, y_recv,
           d_send, d_recv, s_send, s_recv, h_send, y_ready, d_ready):
    layer = lax.axis_index('dep')
    col = lax.axis_index('col')
    row = lax.axis_index('row')
    rows = a_loc.shape[0]
    width = b_full.shape[2]
    copies = rows // CHUNK + 1
    n_x = jnp.where(row == 0, TAKE[0], TAKE[1])
    n_y = copies - n_x
    n_own = jnp.where(row == 0, TAKE[0] - 1, TAKE[1])
    x_peer = (layer, 1 - col, row)
    y_peer = (1 - layer, col, row)
    d_peer = (layer, col, 1 - row)

    barrier = pltpu.get_barrier_semaphore()
    pl.semaphore_signal(barrier, inc=1, device_id=x_peer, device_id_type=MESH)

    @pl.when(layer == 0)
    def _():
        pl.semaphore_signal(barrier, inc=1, device_id=y_peer, device_id_type=MESH)

    @pl.when(row == 1)
    def _():
        pl.semaphore_signal(barrier, inc=1, device_id=d_peer, device_id_type=MESH)

    def span(owner, start, count):
        return pl.ds(pl.multiple_of(start + owner * (rows - 2 * start - count), FIRST), count)

    def place(owner, idx):
        if isinstance(idx, int) and idx == 0:
            return span(owner, 0, FIRST)
        return span(owner, FIRST + (idx - 1) * CHUNK, CHUNK)

    def load_a(start, stop, sem):
        sl = span(layer, start, stop - start)
        return pltpu.make_async_copy(a_hbm.at[sl], a_loc.at[sl], a_sem.at[sem])

    ends = [FIRST + i * CHUNK for i in range(HEAD)] + [FIRST + (NEXT - 1) * CHUNK, rows]
    loads = [load_a(start, stop, sem) for sem, (start, stop) in enumerate(zip([0] + ends, ends))]
    load_b = pltpu.make_async_copy(b_hbm.at[:, pl.ds(pl.multiple_of(layer * width, 128), width)], b_full.at[row], b_sem)

    def send_x(idx):
        sl = place(layer, idx)
        return pltpu.make_async_remote_copy(
            src_ref=a_loc.at[sl], dst_ref=a_rem.at[sl], send_sem=x_send.at[idx], recv_sem=x_recv.at[idx],
            device_id=x_peer, device_id_type=MESH)

    def copy_y(owner, idx):
        sl = place(owner, idx)
        return pltpu.make_async_remote_copy(
            src_ref=a_rem.at[sl], dst_ref=a_rem.at[sl], send_sem=y_send.at[idx], recv_sem=y_recv.at[idx],
            device_id=y_peer, device_id_type=MESH)

    def swap_b(half):
        return pltpu.make_async_remote_copy(
            src_ref=b_full.at[half], dst_ref=b_full.at[half], send_sem=d_send, recv_sem=d_recv,
            device_id=d_peer, device_id_type=MESH)

    helped = TAKE[0] - 1
    hand = pltpu.make_async_remote_copy(
        src_ref=a_hbm.at[place(layer, helped)], dst_ref=stage, send_sem=s_send, recv_sem=s_recv,
        device_id=d_peer, device_id_type=MESH)
    send_help = pltpu.make_async_remote_copy(
        src_ref=stage, dst_ref=a_rem.at[place(layer, helped)], send_sem=h_send, recv_sem=x_recv.at[helped],
        device_id=(layer, 1 - col, 0), device_id_type=MESH)

    for copy in loads[:-1]:
        copy.start()
    load_b.start()
    loads[-1].start()

    pl.semaphore_wait(barrier, 2 + layer - row)

    for i in range(HEAD):
        loads[i].wait()
        send_x(i).start()

    @pl.when(layer == 1)
    def _():
        pl.semaphore_signal(y_ready, inc=1, device_id=y_peer, device_id_type=MESH)

    @pl.when(row == 0)
    def _():
        pl.semaphore_signal(d_ready, inc=1, device_id=d_peer, device_id_type=MESH)

    def launch(i, u):
        send_x(i).start()
        return u

    loads[HEAD].wait()
    lax.fori_loop(HEAD, NEXT, launch, 0)
    load_b.wait()

    @pl.when(row == 1)
    def _():
        pl.semaphore_wait(d_ready, 1)

    swap_b(row).start()

    @pl.when(row == 0)
    def _():
        hand.start()

    loads[-1].wait()
    lax.fori_loop(NEXT, n_own - 1, launch, 0)

    @pl.when(row == 1)
    def _():
        hand.wait_recv()
        send_help.start()

    send_x(n_own - 1).start()

    @pl.when(layer == 0)
    def _():
        pl.semaphore_wait(y_ready, 1)

    def remote(sl):
        c_ref[sl, :] += jnp.dot(a_rem[sl, :], b_full[1 - col], preferred_element_type=jnp.float32)

    def group(owner, idx):
        return span(owner, FIRST + idx * GROUP * CHUNK, GROUP * CHUNK)

    join = WARM + rows // BLOCK
    g_x = (n_x - 2) // GROUP
    g_y = (n_y - 2) // GROUP

    send_x(0).wait_recv()
    copy_y(layer, 0).start()

    def step(i, done):
        x_done, y_done = done

        @pl.when(i < n_x)
        def _():
            send_x(i).wait_recv()

        @pl.when(i < n_y)
        def _():
            copy_y(layer, i).start()

        @pl.when(i == WARM)
        def _():
            swap_b(1 - row).wait_recv()

        @pl.when((i >= WARM) & (i < join))
        def _():
            sl = pl.ds(pl.multiple_of((i - WARM) * BLOCK, BLOCK), BLOCK)
            c_ref[sl, :] = jnp.dot(a_loc[sl, :], b_full[col], preferred_element_type=jnp.float32)

        @pl.when(i == join)
        def _():
            remote(place(layer, 0))
            copy_y(1 - layer, 0).wait_recv()
            remote(place(1 - layer, 0))

        is_x = (i > join) & (x_done < g_x) & ((x_done + 1) * GROUP <= i)
        is_y = (i > join) & (y_done < g_y) & ((y_done + 1) * GROUP + LAG <= i)

        @pl.when(is_x)
        def _():
            remote(group(layer, x_done))

        @pl.when(is_y)
        def _():
            for k in range(GROUP):
                copy_y(1 - layer, y_done * GROUP + k + 1).wait_recv()
            remote(group(1 - layer, y_done))

        return x_done + is_x.astype(jnp.int32), y_done + is_y.astype(jnp.int32)

    lax.fori_loop(1, jnp.maximum(n_x, g_y * GROUP + LAG + 1), step, (0, 0))

    lax.fori_loop(g_y * GROUP + 1, n_y, lambda i, u: (copy_y(1 - layer, i).wait_recv(), u)[1], 0)
    left = rows - 2 * FIRST - sum((t - 2) // GROUP * GROUP * CHUNK for t in (TAKE[0], copies - TAKE[0]))
    remote(span(layer, FIRST + g_x * GROUP * CHUNK, left))

    send_x(0).wait_send()
    copy_y(layer, 0).wait_send()
    lax.fori_loop(1, n_own, lambda i, u: (send_x(i).wait_send(), u)[1], 0)
    lax.fori_loop(1, n_y, lambda i, u: (copy_y(layer, i).wait_send(), u)[1], 0)
    swap_b(row).wait_send()

    @pl.when(row == 0)
    def _():
        hand.wait_send()

    @pl.when(row == 1)
    def _():
        send_help.wait_send()


def solution(mesh):
    n_dep = mesh.shape['dep']

    def local_product(a_blk, b_blk):
        rows, depth = a_blk.shape
        width = b_blk.shape[1] // n_dep
        copies = rows // CHUNK + 1
        return pl.pallas_call(
            kernel,
            out_shape=pltpu.VMEM((rows, width), jnp.float32),
            in_specs=[pl.BlockSpec(memory_space=pltpu.HBM)] * 2,
            out_specs=pl.BlockSpec(memory_space=pltpu.VMEM),
            scratch_shapes=[
                pltpu.VMEM((rows, depth), jnp.bfloat16),
                pltpu.VMEM((rows, depth), jnp.bfloat16),
                pltpu.VMEM((2, depth, width), jnp.bfloat16),
                pltpu.VMEM((CHUNK, depth), jnp.bfloat16),
                pltpu.SemaphoreType.DMA((HEAD + 2,)),
                pltpu.SemaphoreType.DMA,
                pltpu.SemaphoreType.DMA((copies,)),
                pltpu.SemaphoreType.DMA((copies,)),
                pltpu.SemaphoreType.DMA((copies,)),
                pltpu.SemaphoreType.DMA((copies,)),
                pltpu.SemaphoreType.DMA,
                pltpu.SemaphoreType.DMA,
                pltpu.SemaphoreType.DMA,
                pltpu.SemaphoreType.DMA,
                pltpu.SemaphoreType.DMA,
                pltpu.SemaphoreType.REGULAR,
                pltpu.SemaphoreType.REGULAR,
            ],
            compiler_params=pltpu.CompilerParams(collective_id=0, has_side_effects=True, vmem_limit_bytes=40 * 1024 * 1024),
            name='gather_dot',
        )(pltpu.with_memory_space_constraint(a_blk, pltpu.HBM), pltpu.with_memory_space_constraint(b_blk, pltpu.HBM))

    return jax.shard_map(local_product, mesh=mesh, in_specs=(P('row', 'col'), P('row', 'col')), out_specs=P('row', ('col', 'dep')), check_vma=False)
```

time: 62.4 us -> 63.3 us (1.014)
  Pallas kernels: 60.1 us -> 61 us
    pallas_call x1, Pallas kernels: 60.1 us -> 61 us  [local_product(): pl.pallas_call(kernel, out_shape=pltpu.VMEM((rows, width), jnp.float32),...]
where the time goes in v7:
time: 63.3 us; the launch traced here: 63.2 us
  Pallas kernels  61 us (96%)
  local copies, waits for them, and re-layouts  2.19 us (3%)
    pallas_call x1, Pallas kernels, local_product(): pl.pallas_call(kernel, out_shape=pltpu.VMEM((rows, width), jnp.float32),...  61 us
    unnamed x1, local copies, waits for them, and re-layouts  2.19 us

profile of v7, /device:TPU:0, one launch (start us, length us, event | category | flops | bytes accessed | tf_op | source)
XLA Modules:
  0.0 63.2 jit_solution(4814611265107739172)
XLA Ops:
  0.0 61.0 %gather_dot.1 = f32[1536,768]{1,0:T(8,128)S(1)} custom-call(bf16[1536,1536]{1,0:T(8,128)(2,1)} %a_hbm.1, bf16[1536,1536]{1,0:T(8,128)(2,1)} %b_hbm.1), custom_call_target="tpu_custom_call" | custom-call | tf_op jit(solution)/shard_map/gather_dot/pallas_call | solution.py:220
  61.0 2.2 %copy.4 = f32[1536,768]{1,0:T(8,128)} copy(f32[1536,768]{1,0:T(8,128)S(1)} %gather_dot.1) | data formatting | bytes 9437184

commit v8 on v3

--- a/solution.py
+++ b/solution.py
@@ -55,7 +55,7 @@
     def send_x(idx):
         sl = place(layer, idx, 1)
         return pltpu.make_async_remote_copy(
-            src_ref=a_loc.at[sl], dst_ref=a_rem.at[sl], send_sem=x_send.at[idx], recv_sem=x_recv.at[idx],
+            src_ref=a_hbm.at[sl], dst_ref=a_rem.at[sl], send_sem=x_send.at[idx], recv_sem=x_recv.at[idx],
             device_id=x_peer, device_id_type=MESH)
 
     def copy_y(owner, idx):
@@ -77,7 +77,6 @@
     pl.semaphore_wait(barrier, 2 + layer - row)
 
     for i in range(HEAD):
-        loads[i].wait()
         send_x(i).start()
 
     @pl.when(layer == 1)
@@ -92,8 +91,7 @@
         send_x(i).start()
         return u
 
-    loads[HEAD].wait()
-    lax.fori_loop(HEAD, NEXT, launch, 0)
+    lax.fori_loop(HEAD, n_x, launch, 0)
     load_b.wait()
 
     @pl.when(row == 1)
@@ -101,8 +99,8 @@
         pl.semaphore_wait(d_ready, 1)
 
     swap_b(row).start()
-    loads[HEAD + 1].wait()
-    lax.fori_loop(NEXT, n_x, launch, 0)
+    for copy in loads:
+        copy.wait()
 
     @pl.when(layer == 0)
     def _():

time: 62.4 us -> 62 us (level)
  no operation moved by 1% of the time
where the time goes in v8:
time: 62 us; the launch traced here: 61.9 us
  Pallas kernels  59.7 us (96%)
  local copies, waits for them, and re-layouts  2.19 us (4%)
    pallas_call x1, Pallas kernels, local_product(): pl.pallas_call(functools.partial(kernel, n_x, n_y), out_shape=pltpu.VMEM(...  59.7 us
    unnamed x1, local copies, waits for them, and re-layouts  2.19 us

profile of v8, /device:TPU:0, one launch (start us, length us, event | category | flops | bytes accessed | tf_op | source)
XLA Modules:
  0.0 61.9 jit_solution(10318245732183718438)
XLA Ops:
  0.0 59.7 %gather_dot.1 = f32[1536,768]{1,0:T(8,128)S(1)} custom-call(bf16[1536,1536]{1,0:T(8,128)(2,1)} %a_hbm.1, bf16[1536,1536]{1,0:T(8,128)(2,1)} %b_hbm.1), custom_call_target="tpu_custom_call" | custom-call | tf_op jit(solution)/shard_map/gather_dot/pallas_call | solution.py:171
  59.8 2.2 %copy.4 = f32[1536,768]{1,0:T(8,128)} copy(f32[1536,768]{1,0:T(8,128)S(1)} %gather_dot.1) | data formatting | bytes 9437184

commit v9 on v4

--- a/solution.py
+++ b/solution.py
@@ -5,10 +5,11 @@
 from jax.experimental.pallas import tpu as pltpu
 from jax.sharding import PartitionSpec as P
 
-TAKE = (((26, 26), (24, 24)), ((26, 26), (24, 24)))
 MESH = pl.DeviceIdType.MESH
 CHUNK = 32
 GROUP = 64 // CHUNK
+HELP = 1
+TAKE = (25 + HELP, 25)
 LAG = 80 // CHUNK
 HEAD = 64 // CHUNK
 NEXT = 256 // CHUNK
@@ -16,26 +17,16 @@
 WARM = 96 // CHUNK
 
 
-def taken(layer, col, row):
-    total = 0
-    for l in range(2):
-        for j in range(2):
-            for i in range(2):
-                total += TAKE[l][j][i] * (l * layer + (1 - l) * (1 - layer)) * (j * col + (1 - j) * (1 - col)) * (i * row + (1 - i) * (1 - row))
-    return total
-
-
-def kernel(a_hbm, b_hbm, c_ref, a_loc, a_rem, b_full, a_sem, b_sem, x_send, x_recv, y_send, y_recv, d_send, d_recv, y_ready, d_ready):
+def kernel(a_hbm, b_hbm, c_ref, a_loc, a_rem, b_full, stage, a_sem, b_sem, x_send, x_recv, y_send, y_recv, d_send, d_recv, s_send, s_recv, h_send, y_ready, d_ready):
     layer = lax.axis_index('dep')
     col = lax.axis_index('col')
     row = lax.axis_index('row')
     rows = a_loc.shape[0]
     width = b_full.shape[2]
     chunks = rows // CHUNK
-    n_x = taken(layer, col, row)
+    n_x = jnp.where(row == 0, TAKE[0], TAKE[1])
     n_y = chunks - n_x
-    n_out = taken(layer, 1 - col, row)
-    n_pass = chunks - taken(1 - layer, col, row)
+    n_own = jnp.where(row == 0, TAKE[0] - HELP, TAKE[1])
     x_peer = (layer, 1 - col, row)
     y_peer = (1 - layer, col, row)
     d_peer = (layer, col, 1 - row)
@@ -67,7 +58,7 @@
     def send_x(idx):
         sl = place(layer, idx, 1)
         return pltpu.make_async_remote_copy(
-            src_ref=a_loc.at[sl], dst_ref=a_rem.at[sl], send_sem=x_send.at[idx], recv_sem=x_recv.at[idx],
+            src_ref=a_hbm.at[sl], dst_ref=a_rem.at[sl], send_sem=x_send.at[idx], recv_sem=x_recv.at[idx],
             device_id=x_peer, device_id_type=MESH)
 
     def copy_y(owner, idx):
@@ -80,6 +71,17 @@
         return pltpu.make_async_remote_copy(
             src_ref=b_full.at[half], dst_ref=b_full.at[half], send_sem=d_send, recv_sem=d_recv,
             device_id=d_peer, device_id_type=MESH)
+
+    def hand(k):
+        return pltpu.make_async_remote_copy(
+            src_ref=a_hbm.at[place(layer, TAKE[0] - HELP + k, 1)], dst_ref=stage.at[k], send_sem=s_send.at[k], recv_sem=s_recv.at[k],
+            device_id=d_peer, device_id_type=MESH)
+
+    def send_help(k):
+        idx = TAKE[0] - HELP + k
+        return pltpu.make_async_remote_copy(
+            src_ref=stage.at[k], dst_ref=a_rem.at[place(layer, idx, 1)], send_sem=h_send.at[k], recv_sem=x_recv.at[idx],
+            device_id=(layer, 1 - col, 0), device_id_type=MESH)
 
     for copy in loads[:HEAD + 1]:
         copy.start()
@@ -89,7 +91,6 @@
     pl.semaphore_wait(barrier, 2 + layer - row)
 
     for i in range(HEAD):
-        loads[i].wait()
         send_x(i).start()
 
     @pl.when(layer == 1)
@@ -104,8 +105,7 @@
         send_x(i).start()
         return u
 
-    loads[HEAD].wait()
-    lax.fori_loop(HEAD, NEXT, launch, 0)
+    lax.fori_loop(HEAD, jnp.where(row == 0, n_own, n_y), launch, 0)
     load_b.wait()
 
     @pl.when(row == 1)
@@ -113,8 +113,21 @@
         pl.semaphore_wait(d_ready, 1)
 
     swap_b(row).start()
-    loads[HEAD + 1].wait()
-    lax.fori_loop(NEXT, n_out, launch, 0)
+
+    @pl.when(row == 0)
+    def _():
+        for k in range(HELP):
+            hand(k).start()
+
+    @pl.when(row == 1)
+    def _():
+        for k in range(HELP):
+            hand(k).wait_recv()
+            send_help(k).start()
+        lax.fori_loop(n_y, n_own, launch, 0)
+
+    for copy in loads:
+        copy.wait()
 
     @pl.when(layer == 0)
     def _():
@@ -134,7 +147,7 @@
         def _():
             send_x(i).wait_recv()
 
-        @pl.when(i < n_pass)
+        @pl.when(i < n_y)
         def _():
             copy_y(layer, i).start()
 
@@ -170,8 +183,19 @@
     def _():
         remote(place(layer, g_x * GROUP, GROUP))
 
-    lax.fori_loop(0, n_out, lambda i, u: (send_x(i).wait_send(), u)[1], 0)
-    lax.fori_loop(0, n_pass, lambda i, u: (copy_y(layer, i).wait_send(), u)[1], 0)
+    lax.fori_loop(0, n_own, lambda i, u: (send_x(i).wait_send(), u)[1], 0)
+    lax.fori_loop(0, n_y, lambda i, u: (copy_y(layer, i).wait_send(), u)[1], 0)
+
+    @pl.when(row == 0)
+    def _():
+        for k in range(HELP):
+            hand(k).wait_send()
+
+    @pl.when(row == 1)
+    def _():
+        for k in range(HELP):
+            send_help(k).wait_send()
+
     swap_b(row).wait_send()
 
 
@@ -191,6 +215,7 @@
                 pltpu.VMEM((rows, depth), jnp.bfloat16),
                 pltpu.VMEM((rows, depth), jnp.bfloat16),
                 pltpu.VMEM((2, depth, width), jnp.bfloat16),
+                pltpu.VMEM((HELP, CHUNK, depth), jnp.bfloat16),
                 pltpu.SemaphoreType.DMA((HEAD + 2,)),
                 pltpu.SemaphoreType.DMA,
                 pltpu.SemaphoreType.DMA((chunks,)),
@@ -199,6 +224,9 @@
                 pltpu.SemaphoreType.DMA((chunks,)),
                 pltpu.SemaphoreType.DMA,
                 pltpu.SemaphoreType.DMA,
+                pltpu.SemaphoreType.DMA((HELP,)),
+                pltpu.SemaphoreType.DMA((HELP,)),
+                pltpu.SemaphoreType.DMA((HELP,)),
                 pltpu.SemaphoreType.REGULAR,
                 pltpu.SemaphoreType.REGULAR,
             ],

time: 64.6 us -> 62.6 us (0.969)
  Pallas kernels: 62.3 us -> 60.3 us
    pallas_call x1, Pallas kernels: 62.3 us -> 60.3 us  [local_product(): pl.pallas_call(kernel, out_shape=pltpu.VMEM((rows, width), jnp.float32),...]
where the time goes in v9:
time: 62.6 us; the launch traced here: 62.5 us
  Pallas kernels  60.3 us (96%)
  local copies, waits for them, and re-layouts  2.19 us (3%)
    pallas_call x1, Pallas kernels, local_product(): pl.pallas_call(kernel, out_shape=pltpu.VMEM((rows, width), jnp.float32),...  60.3 us
    unnamed x1, local copies, waits for them, and re-layouts  2.19 us

profile of v9, /device:TPU:0, one launch (start us, length us, event | category | flops | bytes accessed | tf_op | source)
XLA Modules:
  0.0 62.5 jit_solution(14814749979985567740)
XLA Ops:
  0.0 60.3 %gather_dot.1 = f32[1536,768]{1,0:T(8,128)S(1)} custom-call(bf16[1536,1536]{1,0:T(8,128)(2,1)} %a_hbm.1, bf16[1536,1536]{1,0:T(8,128)(2,1)} %b_hbm.1), custom_call_target="tpu_custom_call" | custom-call | tf_op jit(solution)/shard_map/gather_dot/pallas_call | solution.py:209
  60.3 2.2 %copy.4 = f32[1536,768]{1,0:T(8,128)} copy(f32[1536,768]{1,0:T(8,128)S(1)} %gather_dot.1) | data formatting | bytes 9437184

commit v10 on v8

--- a/solution.py
+++ b/solution.py
@@ -15,10 +15,11 @@
 HEAD = 64 // CHUNK
 NEXT = 256 // CHUNK
 BLOCK = 256
+START = 0
 WARM = 96 // CHUNK
 
 
-def kernel(n_x, n_y, a_hbm, b_hbm, c_ref, a_loc, a_rem, b_full, a_sem, b_sem, x_send, x_recv, y_send, y_recv, d_send, d_recv, y_ready, d_ready):
+def kernel(n_x, n_y, a_hbm, b_hbm, c_ref, a_loc, a_rem, b_full, a_sem, b_sem, x_send, x_recv, y_send, y_recv, d_send, d_recv, y_ready, d_ready, go):
     layer = lax.axis_index('dep')
     col = lax.axis_index('col')
     row = lax.axis_index('row')
@@ -76,22 +77,22 @@
 
     pl.semaphore_wait(barrier, 2 + layer - row)
 
-    for i in range(HEAD):
-        send_x(i).start()
-
-    @pl.when(layer == 1)
-    def _():
-        pl.semaphore_signal(y_ready, inc=1, device_id=y_peer, device_id_type=MESH)
-
-    @pl.when(row == 0)
-    def _():
-        pl.semaphore_signal(d_ready, inc=1, device_id=d_peer, device_id_type=MESH)
-
     def launch(i, u):
         send_x(i).start()
         return u
 
-    lax.fori_loop(HEAD, n_x, launch, 0)
+    @pl.when(row == 0)
+    def _():
+        lax.fori_loop(0, n_x, launch, 0)
+
+    @pl.when(layer == 1)
+    def _():
+        pl.semaphore_signal(y_ready, inc=1, device_id=y_peer, device_id_type=MESH)
+
+    @pl.when(row == 0)
+    def _():
+        pl.semaphore_signal(d_ready, inc=1, device_id=d_peer, device_id_type=MESH)
+
     load_b.wait()
 
     @pl.when(row == 1)
@@ -102,6 +103,11 @@
     for copy in loads:
         copy.wait()
 
+    @pl.when(row == 1)
+    def _():
+        pl.semaphore_wait(go, 1)
+        lax.fori_loop(0, n_x, launch, 0)
+
     @pl.when(layer == 0)
     def _():
         pl.semaphore_wait(y_ready, 1)
@@ -123,6 +129,10 @@
         @pl.when(i < n_y)
         def _():
             copy_y(layer, i).start()
+
+        @pl.when((i == START) & (row == 0))
+        def _():
+            pl.semaphore_signal(go, inc=1, device_id=d_peer, device_id_type=MESH)
 
         @pl.when(i == WARM)
         def _():
@@ -187,6 +197,7 @@
                 pltpu.SemaphoreType.DMA,
                 pltpu.SemaphoreType.REGULAR,
                 pltpu.SemaphoreType.REGULAR,
+                pltpu.SemaphoreType.REGULAR,
             ],
             compiler_params=pltpu.CompilerParams(collective_id=0, has_side_effects=True, vmem_limit_bytes=40 * 1024 * 1024),
             name='gather_dot',

time: 62 us -> 62.3 us (level)
  the two profiles are of different devices: /device:TPU:0 before, /device:TPU:1 now
where the time goes in v10:
time: 62.3 us; the launch traced here: 62.2 us
  Pallas kernels  60 us (96%)
  local copies, waits for them, and re-layouts  2.19 us (4%)
    pallas_call x1, Pallas kernels, local_product(): pl.pallas_call(functools.partial(kernel, n_x, n_y), out_shape=pltpu.VMEM(...  60 us
    unnamed x1, local copies, waits for them, and re-layouts  2.19 us

profile of v10, /device:TPU:1, one launch (start us, length us, event | category | flops | bytes accessed | tf_op | source)
XLA Modules:
  0.0 62.2 jit_solution(2886052777122199184)
XLA Ops:
  0.0 60.0 %gather_dot.1 = f32[1536,768]{1,0:T(8,128)S(1)} custom-call(bf16[1536,1536]{1,0:T(8,128)(2,1)} %a_hbm.1, bf16[1536,1536]{1,0:T(8,128)(2,1)} %b_hbm.1), custom_call_target="tpu_custom_call" | custom-call | tf_op jit(solution)/shard_map/gather_dot/pallas_call | solution.py:181
  60.0 2.2 %copy.4 = f32[1536,768]{1,0:T(8,128)} copy(f32[1536,768]{1,0:T(8,128)S(1)} %gather_dot.1) | data formatting | bytes 9437184

commit v11 on v10

--- a/solution.py
+++ b/solution.py
@@ -11,11 +11,11 @@
 CHUNK = 32
 GROUP = 64 // CHUNK
 LEAD = 64 // CHUNK
-LAG = 80 // CHUNK
+LAG = 128 // CHUNK
 HEAD = 64 // CHUNK
 NEXT = 256 // CHUNK
 BLOCK = 256
-START = 0
+START = 1
 WARM = 96 // CHUNK
 
 
@@ -100,6 +100,13 @@
         pl.semaphore_wait(d_ready, 1)
 
     swap_b(row).start()
+
+    @pl.when(row == 0)
+    def _():
+        for i in range(START):
+            send_x(i).wait_send()
+        pl.semaphore_signal(go, inc=1, device_id=d_peer, device_id_type=MESH)
+
     for copy in loads:
         copy.wait()
 
@@ -129,10 +136,6 @@
         @pl.when(i < n_y)
         def _():
             copy_y(layer, i).start()
-
-        @pl.when((i == START) & (row == 0))
-        def _():
-            pl.semaphore_signal(go, inc=1, device_id=d_peer, device_id_type=MESH)
 
         @pl.when(i == WARM)
         def _():
@@ -165,7 +168,7 @@
     if n_x % GROUP:
         remote(place(layer, g_x * GROUP, GROUP))
 
-    lax.fori_loop(0, n_x, lambda i, u: (send_x(i).wait_send(), u)[1], 0)
+    lax.fori_loop(jnp.where(row == 0, START, 0), n_x, lambda i, u: (send_x(i).wait_send(), u)[1], 0)
     lax.fori_loop(0, n_y, lambda i, u: (copy_y(layer, i).wait_send(), u)[1], 0)
     swap_b(row).wait_send()
 

time: 62.3 us -> 62.5 us (level)
  no operation moved by 1% of the time
where the time goes in v11:
time: 62.5 us; the launch traced here: 62.4 us
  Pallas kernels  60.2 us (96%)
  local copies, waits for them, and re-layouts  2.19 us (4%)
    pallas_call x1, Pallas kernels, local_product(): pl.pallas_call(functools.partial(kernel, n_x, n_y), out_shape=pltpu.VMEM(...  60.2 us
    unnamed x1, local copies, waits for them, and re-layouts  2.19 us

profile of v11, /device:TPU:1, one launch (start us, length us, event | category | flops | bytes accessed | tf_op | source)
XLA Modules:
  0.0 62.4 jit_solution(14878307245367863420)
XLA Ops:
  0.0 60.2 %gather_dot.1 = f32[1536,768]{1,0:T(8,128)S(1)} custom-call(bf16[1536,1536]{1,0:T(8,128)(2,1)} %a_hbm.1, bf16[1536,1536]{1,0:T(8,128)(2,1)} %b_hbm.1), custom_call_target="tpu_custom_call" | custom-call | tf_op jit(solution)/shard_map/gather_dot/pallas_call | solution.py:184
  60.2 2.2 %copy.4 = f32[1536,768]{1,0:T(8,128)} copy(f32[1536,768]{1,0:T(8,128)S(1)} %gather_dot.1) | data formatting | bytes 9437184

commit v12 on v11

--- a/solution.py
+++ b/solution.py
@@ -1,5 +1,3 @@
-import functools
-
 import jax
 import jax.numpy as jnp
 from jax import lax
@@ -10,21 +8,24 @@
 MESH = pl.DeviceIdType.MESH
 CHUNK = 32
 GROUP = 64 // CHUNK
-LEAD = 64 // CHUNK
-LAG = 128 // CHUNK
+TAKE = (25, 26)
+LAG = 80 // CHUNK
 HEAD = 64 // CHUNK
 NEXT = 256 // CHUNK
 BLOCK = 256
-START = 1
+START = 0
 WARM = 96 // CHUNK
 
 
-def kernel(n_x, n_y, a_hbm, b_hbm, c_ref, a_loc, a_rem, b_full, a_sem, b_sem, x_send, x_recv, y_send, y_recv, d_send, d_recv, y_ready, d_ready, go):
+def kernel(a_hbm, b_hbm, c_ref, a_loc, a_rem, b_full, a_sem, b_sem, x_send, x_recv, y_send, y_recv, d_send, d_recv, y_ready, d_ready, go):
     layer = lax.axis_index('dep')
     col = lax.axis_index('col')
     row = lax.axis_index('row')
     rows = a_loc.shape[0]
     width = b_full.shape[2]
+    chunks = rows // CHUNK
+    n_x = jnp.where(row == 0, TAKE[0], TAKE[1])
+    n_y = chunks - n_x
     x_peer = (layer, 1 - col, row)
     y_peer = (1 - layer, col, row)
     d_peer = (layer, col, 1 - row)
@@ -161,11 +162,12 @@
 
         return x_done + is_x.astype(jnp.int32), y_done + is_y.astype(jnp.int32)
 
-    lax.fori_loop(0, max(n_x, g_y * GROUP + LAG), step, (0, 0))
-
-    for k in range(g_y * GROUP, n_y):
-        copy_y(1 - layer, k).wait_recv()
-    if n_x % GROUP:
+    lax.fori_loop(0, jnp.maximum(n_x, g_y * GROUP + LAG), step, (0, 0))
+
+    lax.fori_loop(g_y * GROUP, n_y, lambda i, u: (copy_y(1 - layer, i).wait_recv(), u)[1], 0)
+
+    @pl.when(g_x + g_y < chunks // GROUP)
+    def _():
         remote(place(layer, g_x * GROUP, GROUP))
 
     lax.fori_loop(jnp.where(row == 0, START, 0), n_x, lambda i, u: (send_x(i).wait_send(), u)[1], 0)
@@ -179,10 +181,9 @@
     def local_product(a_blk, b_blk):
         rows, depth = a_blk.shape
         width = b_blk.shape[1] // n_dep
-        n_x = (rows // CHUNK + LEAD) // 2
-        n_y = n_x - LEAD
+        chunks = rows // CHUNK
         return pl.pallas_call(
-            functools.partial(kernel, n_x, n_y),
+            kernel,
             out_shape=pltpu.VMEM((rows, width), jnp.float32),
             in_specs=[pl.BlockSpec(memory_space=pltpu.HBM)] * 2,
             out_specs=pl.BlockSpec(memory_space=pltpu.VMEM),
@@ -192,10 +193,10 @@
                 pltpu.VMEM((2, depth, width), jnp.bfloat16),
                 pltpu.SemaphoreType.DMA((HEAD + 2,)),
                 pltpu.SemaphoreType.DMA,
-                pltpu.SemaphoreType.DMA((n_x,)),
-                pltpu.SemaphoreType.DMA((n_x,)),
-                pltpu.SemaphoreType.DMA((n_y,)),
-                pltpu.SemaphoreType.DMA((n_y,)),
+                pltpu.SemaphoreType.DMA((chunks,)),
+                pltpu.SemaphoreType.DMA((chunks,)),
+                pltpu.SemaphoreType.DMA((chunks,)),
+                pltpu.SemaphoreType.DMA((chunks,)),
                 pltpu.SemaphoreType.DMA,
                 pltpu.SemaphoreType.DMA,
                 pltpu.SemaphoreType.REGULAR,

time: 62.5 us -> 62.6 us (level)
  the two profiles are of different devices: /device:TPU:1 before, /device:TPU:0 now
where the time goes in v12:
time: 62.6 us; the launch traced here: 61.5 us
  Pallas kernels  59.3 us (95%)
  local copies, waits for them, and re-layouts  2.19 us (3%)
    pallas_call x1, Pallas kernels, local_product(): pl.pallas_call(kernel, out_shape=pltpu.VMEM((rows, width), jnp.float32),...  59.3 us
    unnamed x1, local copies, waits for them, and re-layouts  2.19 us

profile of v12, /device:TPU:0, one launch (start us, length us, event | category | flops | bytes accessed | tf_op | source)
XLA Modules:
  0.0 61.5 jit_solution(10210990237545214694)
XLA Ops:
  0.0 59.3 %gather_dot.1 = f32[1536,768]{1,0:T(8,128)S(1)} custom-call(bf16[1536,1536]{1,0:T(8,128)(2,1)} %a_hbm.1, bf16[1536,1536]{1,0:T(8,128)(2,1)} %b_hbm.1), custom_call_target="tpu_custom_call" | custom-call | tf_op jit(solution)/shard_map/gather_dot/pallas_call | solution.py:185
  59.3 2.2 %copy.4 = f32[1536,768]{1,0:T(8,128)} copy(f32[1536,768]{1,0:T(8,128)S(1)} %gather_dot.1) | data formatting | bytes 9437184

commit v13 on v8

--- a/solution.py
+++ b/solution.py
@@ -18,7 +18,7 @@
 WARM = 96 // CHUNK
 
 
-def kernel(n_x, n_y, a_hbm, b_hbm, c_ref, a_loc, a_rem, b_full, a_sem, b_sem, x_send, x_recv, y_send, y_recv, d_send, d_recv, y_ready, d_ready):
+def kernel(n_x, n_y, a_hbm, b_hbm, c_ref, a_rem, b_full, a_loc, a_sem, b_sem, x_send, x_recv, y_send, y_recv, d_send, d_recv, y_ready, d_ready):
     layer = lax.axis_index('dep')
     col = lax.axis_index('col')
     row = lax.axis_index('row')
@@ -152,12 +152,39 @@
 
     for k in range(g_y * GROUP, n_y):
         copy_y(1 - layer, k).wait_recv()
-    if n_x % GROUP:
-        remote(place(layer, g_x * GROUP, GROUP))
-
     lax.fori_loop(0, n_x, lambda i, u: (send_x(i).wait_send(), u)[1], 0)
     lax.fori_loop(0, n_y, lambda i, u: (copy_y(layer, i).wait_send(), u)[1], 0)
     swap_b(row).wait_send()
+
+
+def finish(n_x, c_ref, a_rem, b_full, out, last, sem):
+    layer = lax.axis_index('dep')
+    col = lax.axis_index('col')
+    rows = a_rem.shape[0]
+    size = GROUP * CHUNK
+    count = rows // size
+    mine = n_x // GROUP + layer * (count - 1 - 2 * (n_x // GROUP))
+
+    def block(i):
+        return pl.ds(pl.multiple_of(i * size, size), size)
+
+    def put(i):
+        return pltpu.make_async_copy(c_ref.at[block(i)], out.at[block(i)], sem)
+
+    def put_last():
+        return pltpu.make_async_copy(last, out.at[block(mine)], sem)
+
+    def start(i, u):
+        @pl.when(i != mine)
+        def _():
+            put(i).start()
+
+        return u
+
+    lax.fori_loop(0, count, start, 0)
+    last[...] = c_ref[block(mine), :] + jnp.dot(a_rem[block(mine), :], b_full[1 - col], preferred_element_type=jnp.float32)
+    put_last().start()
+    pltpu.make_async_copy(c_ref, out, sem).wait()
 
 
 def solution(mesh):
@@ -168,15 +195,17 @@
         width = b_blk.shape[1] // n_dep
         n_x = (rows // CHUNK + LEAD) // 2
         n_y = n_x - LEAD
-        return pl.pallas_call(
+        c, a_rem, b_full = pl.pallas_call(
             functools.partial(kernel, n_x, n_y),
-            out_shape=pltpu.VMEM((rows, width), jnp.float32),
+            out_shape=(
+                pltpu.VMEM((rows, width), jnp.float32),
+                pltpu.VMEM((rows, depth), jnp.bfloat16),
+                pltpu.VMEM((2, depth, width), jnp.bfloat16),
+            ),
             in_specs=[pl.BlockSpec(memory_space=pltpu.HBM)] * 2,
-            out_specs=pl.BlockSpec(memory_space=pltpu.VMEM),
+            out_specs=(pl.BlockSpec(memory_space=pltpu.VMEM),) * 3,
             scratch_shapes=[
                 pltpu.VMEM((rows, depth), jnp.bfloat16),
-                pltpu.VMEM((rows, depth), jnp.bfloat16),
-                pltpu.VMEM((2, depth, width), jnp.bfloat16),
                 pltpu.SemaphoreType.DMA((HEAD + 2,)),
                 pltpu.SemaphoreType.DMA,
                 pltpu.SemaphoreType.DMA((n_x,)),
@@ -192,4 +221,14 @@
             name='gather_dot',
         )(pltpu.with_memory_space_constraint(a_blk, pltpu.HBM), pltpu.with_memory_space_constraint(b_blk, pltpu.HBM))
 
+        return pl.pallas_call(
+            functools.partial(finish, n_x),
+            out_shape=pltpu.HBM((rows, width), jnp.float32),
+            in_specs=[pl.BlockSpec(memory_space=pltpu.VMEM)] * 3,
+            out_specs=pl.BlockSpec(memory_space=pltpu.HBM),
+            scratch_shapes=[pltpu.VMEM((GROUP * CHUNK, width), jnp.float32), pltpu.SemaphoreType.DMA],
+            compiler_params=pltpu.CompilerParams(vmem_limit_bytes=8 * 1024 * 1024),
+            name='finish',
+        )(*(pltpu.with_memory_space_constraint(v, pltpu.VMEM) for v in (c, a_rem, b_full)))
+
     return jax.shard_map(local_product, mesh=mesh, in_specs=(P('row', 'col'), P('row', 'col')), out_specs=P('row', ('col', 'dep')), check_vma=False)

time: 62 us -> 61.4 us (level)
  local copies, waits for them, and re-layouts: 2.19 us -> 0 us
  Pallas kernels: 59.7 us -> 61.3 us
    unnamed x1 -> x0, local copies, waits for them, and re-layouts: 2.19 us -> none
    pallas_call x1 -> x2, Pallas kernels: 59.7 us -> 61.3 us  [the longest x1 59.2 us: local_product(): pl.pallas_call(functools.partial(kernel, n_x, n_y), out_shape=(pltpu.VMEM...]
where the time goes in v13:
time: 61.4 us
  Pallas kernels  61.3 us (100%)
    pallas_call x1, Pallas kernels, local_product(): pl.pallas_call(functools.partial(kernel, n_x, n_y), out_shape=(pltpu.VMEM...  59.2 us
    pallas_call x1, Pallas kernels, local_product(): pl.pallas_call(functools.partial(finish, n_x), out_shape=pltpu.HBM((rows,...  2.17 us

profile of v13, /device:TPU:0, one launch (start us, length us, event | category | flops | bytes accessed | tf_op | source)
XLA Modules:
  0.0 61.4 jit_solution(11889871195381735071)
XLA Ops:
  0.0 59.2 %gather_dot.1 = (f32[1536,768]{1,0:T(8,128)S(1)}, bf16[1536,1536]{1,0:T(8,128)(2,1)S(1)}, bf16[2,1536,768]{2,1,0:T(8,128)(2,1)S(1)}) custom-call(bf16[1536,1536]{1,0:T(8,128)(2,1)} %a_hbm.1, bf16[1536,1536]{1,0:T(8,128)(2,1)} %b_hbm.1), custom_call_target="tpu_custom_call" | custom-call | tf_op jit(solution)/shard_map/gather_dot/pallas_call | solution.py:198
  59.2 2.2 %finish.1 = f32[1536,768]{1,0:T(8,128)} custom-call(f32[1536,768]{1,0:T(8,128)S(1)} %get-tuple-element.8.c_ref, bf16[1536,1536]{1,0:T(8,128)(2,1)S(1)} %get-tuple-element.9.a_rem, bf16[2,1536,768]{2,1,0:T(8,128)(2,1)S(1)} %get-tuple-element.10.b_full), custom_call_target="tpu_custom_call" | custom-call | tf_op jit(solution)/shard_map/finish/pallas_call | solution.py:224

commit v14 on v13

--- a/solution.py
+++ b/solution.py
@@ -10,7 +10,8 @@
 MESH = pl.DeviceIdType.MESH
 CHUNK = 32
 GROUP = 64 // CHUNK
-LEAD = 64 // CHUNK
+LEAD = 96 // CHUNK
+HALF = CHUNK // 2
 LAG = 80 // CHUNK
 HEAD = 64 // CHUNK
 NEXT = 256 // CHUNK
@@ -43,6 +44,10 @@
         start = idx * CHUNK + owner * (rows - (2 * idx + count) * CHUNK)
         return pl.ds(pl.multiple_of(start, CHUNK), count * CHUNK)
 
+    def half(owner, idx):
+        start = idx * CHUNK
+        return pl.ds(pl.multiple_of(start + owner * (rows - 2 * start - HALF), HALF), HALF)
+
     def load_a(idx, count, sem):
         sl = place(layer, idx, count)
         return pltpu.make_async_copy(a_hbm.at[sl], a_loc.at[sl], a_sem.at[sem])
@@ -64,9 +69,19 @@
             src_ref=a_rem.at[sl], dst_ref=a_rem.at[sl], send_sem=y_send.at[idx], recv_sem=y_recv.at[idx],
             device_id=y_peer, device_id_type=MESH)
 
-    def swap_b(half):
-        return pltpu.make_async_remote_copy(
-            src_ref=b_full.at[half], dst_ref=b_full.at[half], send_sem=d_send, recv_sem=d_recv,
+    half_x = pltpu.make_async_remote_copy(
+        src_ref=a_hbm.at[half(layer, n_x)], dst_ref=a_rem.at[half(layer, n_x)], send_sem=x_send.at[n_x], recv_sem=x_recv.at[n_x],
+        device_id=x_peer, device_id_type=MESH)
+
+    def half_y(owner):
+        sl = half(owner, n_y)
+        return pltpu.make_async_remote_copy(
+            src_ref=a_rem.at[sl], dst_ref=a_rem.at[sl], send_sem=y_send.at[n_y], recv_sem=y_recv.at[n_y],
+            device_id=y_peer, device_id_type=MESH)
+
+    def swap_b(side):
+        return pltpu.make_async_remote_copy(
+            src_ref=b_full.at[side], dst_ref=b_full.at[side], send_sem=d_send, recv_sem=d_recv,
             device_id=d_peer, device_id_type=MESH)
 
     for copy in loads[:HEAD + 1]:
@@ -92,6 +107,7 @@
         return u
 
     lax.fori_loop(HEAD, n_x, launch, 0)
+    half_x.start()
     load_b.wait()
 
     @pl.when(row == 1)
@@ -124,6 +140,10 @@
         def _():
             copy_y(layer, i).start()
 
+        @pl.when(i == n_y)
+        def _():
+            half_y(layer).start()
+
         @pl.when(i == WARM)
         def _():
             swap_b(1 - row).wait_recv()
@@ -152,8 +172,13 @@
 
     for k in range(g_y * GROUP, n_y):
         copy_y(1 - layer, k).wait_recv()
+    half_x.wait_recv()
+    half_y(1 - layer).wait_recv()
+
     lax.fori_loop(0, n_x, lambda i, u: (send_x(i).wait_send(), u)[1], 0)
     lax.fori_loop(0, n_y, lambda i, u: (copy_y(layer, i).wait_send(), u)[1], 0)
+    half_x.wait_send()
+    half_y(layer).wait_send()
     swap_b(row).wait_send()
 
 
@@ -193,7 +218,7 @@
     def local_product(a_blk, b_blk):
         rows, depth = a_blk.shape
         width = b_blk.shape[1] // n_dep
-        n_x = (rows // CHUNK + LEAD) // 2
+        n_x = (rows // CHUNK + LEAD - 1) // 2
         n_y = n_x - LEAD
         c, a_rem, b_full = pl.pallas_call(
             functools.partial(kernel, n_x, n_y),
@@ -208,10 +233,10 @@
                 pltpu.VMEM((rows, depth), jnp.bfloat16),
                 pltpu.SemaphoreType.DMA((HEAD + 2,)),
                 pltpu.SemaphoreType.DMA,
-                pltpu.SemaphoreType.DMA((n_x,)),
-                pltpu.SemaphoreType.DMA((n_x,)),
-                pltpu.SemaphoreType.DMA((n_y,)),
-                pltpu.SemaphoreType.DMA((n_y,)),
+                pltpu.SemaphoreType.DMA((n_x + 1,)),
+                pltpu.SemaphoreType.DMA((n_x + 1,)),
+                pltpu.SemaphoreType.DMA((n_y + 1,)),
+                pltpu.SemaphoreType.DMA((n_y + 1,)),
                 pltpu.SemaphoreType.DMA,
                 pltpu.SemaphoreType.DMA,
                 pltpu.SemaphoreType.REGULAR,

time: 61.4 us -> 61.2 us (level)
  no operation moved by 1% of the time
where the time goes in v14:
time: 61.2 us
  Pallas kernels  61.1 us (100%)
    pallas_call x1, Pallas kernels, local_product(): pl.pallas_call(functools.partial(kernel, n_x, n_y), out_shape=(pltpu.VMEM...  59 us
    pallas_call x1, Pallas kernels, local_product(): pl.pallas_call(functools.partial(finish, n_x), out_shape=pltpu.HBM((rows,...  2.17 us

profile of v14, /device:TPU:0, one launch (start us, length us, event | category | flops | bytes accessed | tf_op | source)
XLA Modules:
  0.0 61.2 jit_solution(14443013615497997129)
XLA Ops:
  0.0 59.0 %gather_dot.1 = (f32[1536,768]{1,0:T(8,128)S(1)}, bf16[1536,1536]{1,0:T(8,128)(2,1)S(1)}, bf16[2,1536,768]{2,1,0:T(8,128)(2,1)S(1)}) custom-call(bf16[1536,1536]{1,0:T(8,128)(2,1)} %a_hbm.1, bf16[1536,1536]{1,0:T(8,128)(2,1)} %b_hbm.1), custom_call_target="tpu_custom_call" | custom-call | tf_op jit(solution)/shard_map/gather_dot/pallas_call | solution.py:223
  59.0 2.2 %finish.1 = f32[1536,768]{1,0:T(8,128)} custom-call(f32[1536,768]{1,0:T(8,128)S(1)} %get-tuple-element.8.c_ref, bf16[1536,1536]{1,0:T(8,128)(2,1)S(1)} %get-tuple-element.9.a_rem, bf16[2,1536,768]{2,1,0:T(8,128)(2,1)S(1)} %get-tuple-element.10.b_full), custom_call_target="tpu_custom_call" | custom-call | tf_op jit(solution)/shard_map/finish/pallas_call | solution.py:249

commit v15 on v14

--- a/solution.py
+++ b/solution.py
@@ -16,6 +16,7 @@
 HEAD = 64 // CHUNK
 NEXT = 256 // CHUNK
 BLOCK = 256
+HOLD = 21
 WARM = 96 // CHUNK
 
 
@@ -106,8 +107,13 @@
         send_x(i).start()
         return u
 
-    lax.fori_loop(HEAD, n_x, launch, 0)
-    half_x.start()
+    first_out = jnp.where(row == 0, n_x, HOLD)
+    lax.fori_loop(HEAD, first_out, launch, 0)
+
+    @pl.when(row == 0)
+    def _():
+        half_x.start()
+
     load_b.wait()
 
     @pl.when(row == 1)
@@ -143,6 +149,11 @@
         @pl.when(i == n_y)
         def _():
             half_y(layer).start()
+
+        @pl.when((i == HOLD - 1) & (row == 1))
+        def _():
+            lax.fori_loop(first_out, n_x, launch, 0)
+            half_x.start()
 
         @pl.when(i == WARM)
         def _():

time: 61.2 us -> 60.2 us (0.984)
  Pallas kernels: 61.1 us -> 59.7 us
    pallas_call x1, Pallas kernels: 59 us -> 57.6 us  [local_product(): pl.pallas_call(functools.partial(kernel, n_x, n_y), out_shape=(pltpu.VMEM...]
where the time goes in v15:
time: 60.2 us; the launch traced here: 59.7 us
  Pallas kernels  59.7 us (99%)
    pallas_call x1, Pallas kernels, local_product(): pl.pallas_call(functools.partial(kernel, n_x, n_y), out_shape=(pltpu.VMEM...  57.6 us
    pallas_call x1, Pallas kernels, local_product(): pl.pallas_call(functools.partial(finish, n_x), out_shape=pltpu.HBM((rows,...  2.17 us

profile of v15, /device:TPU:0, one launch (start us, length us, event | category | flops | bytes accessed | tf_op | source)
XLA Modules:
  0.0 59.7 jit_solution(9041836949492111926)
XLA Ops:
  0.0 57.6 %gather_dot.1 = (f32[1536,768]{1,0:T(8,128)S(1)}, bf16[1536,1536]{1,0:T(8,128)(2,1)S(1)}, bf16[2,1536,768]{2,1,0:T(8,128)(2,1)S(1)}) custom-call(bf16[1536,1536]{1,0:T(8,128)(2,1)} %a_hbm.1, bf16[1536,1536]{1,0:T(8,128)(2,1)} %b_hbm.1), custom_call_target="tpu_custom_call" | custom-call | tf_op jit(solution)/shard_map/gather_dot/pallas_call | solution.py:234
  57.6 2.2 %finish.1 = f32[1536,768]{1,0:T(8,128)} custom-call(f32[1536,768]{1,0:T(8,128)S(1)} %get-tuple-element.8.c_ref, bf16[1536,1536]{1,0:T(8,128)(2,1)S(1)} %get-tuple-element.9.a_rem, bf16[2,1536,768]{2,1,0:T(8,128)(2,1)S(1)} %get-tuple-element.10.b_full), custom_call_target="tpu_custom_call" | custom-call | tf_op jit(solution)/shard_map/finish/pallas_call | solution.py:260

commit v16 on v15

--- a/solution.py
+++ b/solution.py
@@ -146,14 +146,17 @@
         def _():
             copy_y(layer, i).start()
 
-        @pl.when(i == n_y)
+        @pl.when((i == n_y) & (row == 0))
         def _():
             half_y(layer).start()
 
+        @pl.when((i == n_y) & (row == 1))
+        def _():
+            copy_y(layer, n_y).start()
+
         @pl.when((i == HOLD - 1) & (row == 1))
         def _():
             lax.fori_loop(first_out, n_x, launch, 0)
-            half_x.start()
 
         @pl.when(i == WARM)
         def _():
@@ -183,13 +186,27 @@
 
     for k in range(g_y * GROUP, n_y):
         copy_y(1 - layer, k).wait_recv()
-    half_x.wait_recv()
-    half_y(1 - layer).wait_recv()
+    @pl.when(row == 0)
+    def _():
+        half_x.wait_recv()
+        half_y(1 - layer).wait_recv()
+
+    @pl.when(row == 1)
+    def _():
+        copy_y(1 - layer, n_y).wait_recv()
 
     lax.fori_loop(0, n_x, lambda i, u: (send_x(i).wait_send(), u)[1], 0)
     lax.fori_loop(0, n_y, lambda i, u: (copy_y(layer, i).wait_send(), u)[1], 0)
-    half_x.wait_send()
-    half_y(layer).wait_send()
+
+    @pl.when(row == 0)
+    def _():
+        half_x.wait_send()
+        half_y(layer).wait_send()
+
+    @pl.when(row == 1)
+    def _():
+        copy_y(layer, n_y).wait_send()
+
     swap_b(row).wait_send()
 
 

time: 60.2 us -> 60.1 us (level)
  no operation moved by 1% of the time
where the time goes in v16:
time: 60.1 us; the launch traced here: 59.6 us
  Pallas kernels  59.6 us (99%)
    pallas_call x1, Pallas kernels, local_product(): pl.pallas_call(functools.partial(kernel, n_x, n_y), out_shape=(pltpu.VMEM...  57.4 us
    pallas_call x1, Pallas kernels, local_product(): pl.pallas_call(functools.partial(finish, n_x), out_shape=pltpu.HBM((rows,...  2.17 us

profile of v16, /device:TPU:0, one launch (start us, length us, event | category | flops | bytes accessed | tf_op | source)
XLA Modules:
  0.0 59.6 jit_solution(8632628878659686021)
XLA Ops:
  0.0 57.4 %gather_dot.1 = (f32[1536,768]{1,0:T(8,128)S(1)}, bf16[1536,1536]{1,0:T(8,128)(2,1)S(1)}, bf16[2,1536,768]{2,1,0:T(8,128)(2,1)S(1)}) custom-call(bf16[1536,1536]{1,0:T(8,128)(2,1)} %a_hbm.1, bf16[1536,1536]{1,0:T(8,128)(2,1)} %b_hbm.1), custom_call_target="tpu_custom_call" | custom-call | tf_op jit(solution)/shard_map/gather_dot/pallas_call | solution.py:251
  57.4 2.2 %finish.1 = f32[1536,768]{1,0:T(8,128)} custom-call(f32[1536,768]{1,0:T(8,128)S(1)} %get-tuple-element.8.c_ref, bf16[1536,1536]{1,0:T(8,128)(2,1)S(1)} %get-tuple-element.9.a_rem, bf16[2,1536,768]{2,1,0:T(8,128)(2,1)S(1)} %get-tuple-element.10.b_full), custom_call_target="tpu_custom_call" | custom-call | tf_op jit(solution)/shard_map/finish/pallas_call | solution.py:277

commit v17 on v16

--- a/solution.py
+++ b/solution.py
@@ -16,7 +16,7 @@
 HEAD = 64 // CHUNK
 NEXT = 256 // CHUNK
 BLOCK = 256
-HOLD = 21
+HOLD = 23
 WARM = 96 // CHUNK
 
 
@@ -70,9 +70,13 @@
             src_ref=a_rem.at[sl], dst_ref=a_rem.at[sl], send_sem=y_send.at[idx], recv_sem=y_recv.at[idx],
             device_id=y_peer, device_id_type=MESH)
 
-    half_x = pltpu.make_async_remote_copy(
-        src_ref=a_hbm.at[half(layer, n_x)], dst_ref=a_rem.at[half(layer, n_x)], send_sem=x_send.at[n_x], recv_sem=x_recv.at[n_x],
-        device_id=x_peer, device_id_type=MESH)
+    def part_x(start, sem):
+        sl = pl.ds(pl.multiple_of(start + layer * (rows - 2 * start - HALF), HALF), HALF)
+        return pltpu.make_async_remote_copy(
+            src_ref=a_hbm.at[sl], dst_ref=a_rem.at[sl], send_sem=x_send.at[sem], recv_sem=x_recv.at[sem],
+            device_id=x_peer, device_id_type=MESH)
+
+    parts = [part_x(n_y * CHUNK, n_y), part_x(n_y * CHUNK + HALF, n_x + 1), part_x(n_x * CHUNK, n_x)]
 
     def half_y(owner):
         sl = half(owner, n_y)
@@ -107,12 +111,17 @@
         send_x(i).start()
         return u
 
-    first_out = jnp.where(row == 0, n_x, HOLD)
-    lax.fori_loop(HEAD, first_out, launch, 0)
-
     @pl.when(row == 0)
     def _():
-        half_x.start()
+        lax.fori_loop(HEAD, n_y, launch, 0)
+        parts[0].start()
+        parts[1].start()
+        lax.fori_loop(n_y + 1, n_x, launch, 0)
+        parts[2].start()
+
+    @pl.when(row == 1)
+    def _():
+        lax.fori_loop(HEAD, HOLD, launch, 0)
 
     load_b.wait()
 
@@ -138,7 +147,7 @@
     def step(i, done):
         x_done, y_done = done
 
-        @pl.when(i < n_x)
+        @pl.when((i < n_x) & ((i != n_y) | (row == 1)))
         def _():
             send_x(i).wait_recv()
 
@@ -148,7 +157,9 @@
 
         @pl.when((i == n_y) & (row == 0))
         def _():
+            parts[0].wait_recv()
             half_y(layer).start()
+            parts[1].wait_recv()
 
         @pl.when((i == n_y) & (row == 1))
         def _():
@@ -156,7 +167,7 @@
 
         @pl.when((i == HOLD - 1) & (row == 1))
         def _():
-            lax.fori_loop(first_out, n_x, launch, 0)
+            lax.fori_loop(HOLD, n_x, launch, 0)
 
         @pl.when(i == WARM)
         def _():
@@ -188,23 +199,26 @@
         copy_y(1 - layer, k).wait_recv()
     @pl.when(row == 0)
     def _():
-        half_x.wait_recv()
+        parts[2].wait_recv()
         half_y(1 - layer).wait_recv()
 
     @pl.when(row == 1)
     def _():
         copy_y(1 - layer, n_y).wait_recv()
 
-    lax.fori_loop(0, n_x, lambda i, u: (send_x(i).wait_send(), u)[1], 0)
+    lax.fori_loop(0, n_y, lambda i, u: (send_x(i).wait_send(), u)[1], 0)
+    lax.fori_loop(n_y + 1, n_x, lambda i, u: (send_x(i).wait_send(), u)[1], 0)
     lax.fori_loop(0, n_y, lambda i, u: (copy_y(layer, i).wait_send(), u)[1], 0)
 
     @pl.when(row == 0)
     def _():
-        half_x.wait_send()
+        for part in parts:
+            part.wait_send()
         half_y(layer).wait_send()
 
     @pl.when(row == 1)
     def _():
+        send_x(n_y).wait_send()
         copy_y(layer, n_y).wait_send()
 
     swap_b(row).wait_send()
@@ -261,8 +275,8 @@
                 pltpu.VMEM((rows, depth), jnp.bfloat16),
                 pltpu.SemaphoreType.DMA((HEAD + 2,)),
                 pltpu.SemaphoreType.DMA,
-                pltpu.SemaphoreType.DMA((n_x + 1,)),
-                pltpu.SemaphoreType.DMA((n_x + 1,)),
+                pltpu.SemaphoreType.DMA((n_x + 2,)),
+                pltpu.SemaphoreType.DMA((n_x + 2,)),
                 pltpu.SemaphoreType.DMA((n_y + 1,)),
                 pltpu.SemaphoreType.DMA((n_y + 1,)),
                 pltpu.SemaphoreType.DMA,

time: 60.1 us -> 60.3 us (level)
    pallas_call x1, Pallas kernels: 57.4 us -> 58 us  [local_product(): pl.pallas_call(functools.partial(kernel, n_x, n_y), out_shape=(pltpu.VMEM...]
where the time goes in v17:
time: 60.3 us; the launch traced here: 60.2 us
  Pallas kernels  60.2 us (100%)
    pallas_call x1, Pallas kernels, local_product(): pl.pallas_call(functools.partial(kernel, n_x, n_y), out_shape=(pltpu.VMEM...  58 us
    pallas_call x1, Pallas kernels, local_product(): pl.pallas_call(functools.partial(finish, n_x), out_shape=pltpu.HBM((rows,...  2.17 us

profile of v17, /device:TPU:0, one launch (start us, length us, event | category | flops | bytes accessed | tf_op | source)
XLA Modules:
  0.0 60.2 jit_solution(5176337168022044446)
XLA Ops:
  0.0 58.0 %gather_dot.1 = (f32[1536,768]{1,0:T(8,128)S(1)}, bf16[1536,1536]{1,0:T(8,128)(2,1)S(1)}, bf16[2,1536,768]{2,1,0:T(8,128)(2,1)S(1)}) custom-call(bf16[1536,1536]{1,0:T(8,128)(2,1)} %a_hbm.1, bf16[1536,1536]{1,0:T(8,128)(2,1)} %b_hbm.1), custom_call_target="tpu_custom_call" | custom-call | tf_op jit(solution)/shard_map/gather_dot/pallas_call | solution.py:265
  58.0 2.2 %finish.1 = f32[1536,768]{1,0:T(8,128)} custom-call(f32[1536,768]{1,0:T(8,128)S(1)} %get-tuple-element.8.c_ref, bf16[1536,1536]{1,0:T(8,128)(2,1)S(1)} %get-tuple-element.9.a_rem, bf16[2,1536,768]{2,1,0:T(8,128)(2,1)S(1)} %get-tuple-element.10.b_full), custom_call_target="tpu_custom_call" | custom-call | tf_op jit(solution)/shard_map/finish/pallas_call | solution.py:291

commit v18 on v15

--- a/solution.py
+++ b/solution.py
@@ -26,6 +26,8 @@
     row = lax.axis_index('row')
     rows = a_loc.shape[0]
     width = b_full.shape[2]
+    n_full = n_x - row
+    n_pass = n_y + row
     x_peer = (layer, 1 - col, row)
     y_peer = (1 - layer, col, row)
     d_peer = (layer, col, 1 - row)
@@ -71,13 +73,13 @@
             device_id=y_peer, device_id_type=MESH)
 
     half_x = pltpu.make_async_remote_copy(
-        src_ref=a_hbm.at[half(layer, n_x)], dst_ref=a_rem.at[half(layer, n_x)], send_sem=x_send.at[n_x], recv_sem=x_recv.at[n_x],
+        src_ref=a_hbm.at[half(layer, n_full)], dst_ref=a_rem.at[half(layer, n_full)], send_sem=x_send.at[n_full], recv_sem=x_recv.at[n_full],
         device_id=x_peer, device_id_type=MESH)
 
     def half_y(owner):
-        sl = half(owner, n_y)
-        return pltpu.make_async_remote_copy(
-            src_ref=a_rem.at[sl], dst_ref=a_rem.at[sl], send_sem=y_send.at[n_y], recv_sem=y_recv.at[n_y],
+        sl = half(owner, n_pass)
+        return pltpu.make_async_remote_copy(
+            src_ref=a_rem.at[sl], dst_ref=a_rem.at[sl], send_sem=y_send.at[n_pass], recv_sem=y_recv.at[n_pass],
             device_id=y_peer, device_id_type=MESH)
 
     def swap_b(side):
@@ -107,7 +109,7 @@
         send_x(i).start()
         return u
 
-    first_out = jnp.where(row == 0, n_x, HOLD)
+    first_out = jnp.where(row == 0, n_full, HOLD)
     lax.fori_loop(HEAD, first_out, launch, 0)
 
     @pl.when(row == 0)
@@ -138,21 +140,21 @@
     def step(i, done):
         x_done, y_done = done
 
-        @pl.when(i < n_x)
+        @pl.when(i < n_full)
         def _():
             send_x(i).wait_recv()
 
-        @pl.when(i < n_y)
+        @pl.when(i < n_pass)
         def _():
             copy_y(layer, i).start()
 
-        @pl.when(i == n_y)
+        @pl.when(i == n_pass)
         def _():
             half_y(layer).start()
 
         @pl.when((i == HOLD - 1) & (row == 1))
         def _():
-            lax.fori_loop(first_out, n_x, launch, 0)
+            lax.fori_loop(first_out, n_full, launch, 0)
             half_x.start()
 
         @pl.when(i == WARM)
@@ -181,13 +183,12 @@
 
     lax.fori_loop(0, max(n_x, g_y * GROUP + LAG), step, (0, 0))
 
-    for k in range(g_y * GROUP, n_y):
-        copy_y(1 - layer, k).wait_recv()
+    lax.fori_loop(g_y * GROUP, n_pass, lambda i, u: (copy_y(1 - layer, i).wait_recv(), u)[1], 0)
     half_x.wait_recv()
     half_y(1 - layer).wait_recv()
 
-    lax.fori_loop(0, n_x, lambda i, u: (send_x(i).wait_send(), u)[1], 0)
-    lax.fori_loop(0, n_y, lambda i, u: (copy_y(layer, i).wait_send(), u)[1], 0)
+    lax.fori_loop(0, n_full, lambda i, u: (send_x(i).wait_send(), u)[1], 0)
+    lax.fori_loop(0, n_pass, lambda i, u: (copy_y(layer, i).wait_send(), u)[1], 0)
     half_x.wait_send()
     half_y(layer).wait_send()
     swap_b(row).wait_send()
@@ -246,8 +247,8 @@
                 pltpu.SemaphoreType.DMA,
                 pltpu.SemaphoreType.DMA((n_x + 1,)),
                 pltpu.SemaphoreType.DMA((n_x + 1,)),
-                pltpu.SemaphoreType.DMA((n_y + 1,)),
-                pltpu.SemaphoreType.DMA((n_y + 1,)),
+                pltpu.SemaphoreType.DMA((n_y + 2,)),
+                pltpu.SemaphoreType.DMA((n_y + 2,)),
                 pltpu.SemaphoreType.DMA,
                 pltpu.SemaphoreType.DMA,
                 pltpu.SemaphoreType.REGULAR,

time: 60.2 us -> 61.7 us (1.025)
  the two profiles are of different devices: /device:TPU:0 before, /device:TPU:1 now
where the time goes in v18:
time: 61.7 us; the launch traced here: 61.6 us
  Pallas kernels  61.6 us (100%)
    pallas_call x1, Pallas kernels, local_product(): pl.pallas_call(functools.partial(kernel, n_x, n_y), out_shape=(pltpu.VMEM...  59.5 us
    pallas_call x1, Pallas kernels, local_product(): pl.pallas_call(functools.partial(finish, n_x), out_shape=pltpu.HBM((rows,...  2.17 us

profile of v18, /device:TPU:1, one launch (start us, length us, event | category | flops | bytes accessed | tf_op | source)
XLA Modules:
  0.0 61.6 jit_solution(14329516159487082508)
XLA Ops:
  0.0 59.5 %gather_dot.1 = (f32[1536,768]{1,0:T(8,128)S(1)}, bf16[1536,1536]{1,0:T(8,128)(2,1)S(1)}, bf16[2,1536,768]{2,1,0:T(8,128)(2,1)S(1)}) custom-call(bf16[1536,1536]{1,0:T(8,128)(2,1)} %a_hbm.1, bf16[1536,1536]{1,0:T(8,128)(2,1)} %b_hbm.1), custom_call_target="tpu_custom_call" | custom-call | tf_op jit(solution)/shard_map/gather_dot/pallas_call | solution.py:235
  59.5 2.2 %finish.1 = f32[1536,768]{1,0:T(8,128)} custom-call(f32[1536,768]{1,0:T(8,128)S(1)} %get-tuple-element.8.c_ref, bf16[1536,1536]{1,0:T(8,128)(2,1)S(1)} %get-tuple-element.9.a_rem, bf16[2,1536,768]{2,1,0:T(8,128)(2,1)S(1)} %get-tuple-element.10.b_full), custom_call_target="tpu_custom_call" | custom-call | tf_op jit(solution)/shard_map/finish/pallas_call | solution.py:261

commit v19 on v13

--- a/solution.py
+++ b/solution.py
@@ -15,6 +15,7 @@
 HEAD = 64 // CHUNK
 NEXT = 256 // CHUNK
 BLOCK = 256
+HOLD = 21
 WARM = 96 // CHUNK
 
 
@@ -91,7 +92,8 @@
         send_x(i).start()
         return u
 
-    lax.fori_loop(HEAD, n_x, launch, 0)
+    first_out = jnp.where(row == 0, n_x, HOLD)
+    lax.fori_loop(HEAD, first_out, launch, 0)
     load_b.wait()
 
     @pl.when(row == 1)
@@ -123,6 +125,10 @@
         @pl.when(i < n_y)
         def _():
             copy_y(layer, i).start()
+
+        @pl.when((i == HOLD - 1) & (row == 1))
+        def _():
+            lax.fori_loop(HOLD, n_x, launch, 0)
 
         @pl.when(i == WARM)
         def _():

time: 61.4 us -> 60 us (0.977)
  Pallas kernels: 61.3 us -> 59.9 us
    pallas_call x1, Pallas kernels: 59.2 us -> 57.7 us  [local_product(): pl.pallas_call(functools.partial(kernel, n_x, n_y), out_shape=(pltpu.VMEM...]
where the time goes in v19:
time: 60 us; the launch traced here: 59.9 us
  Pallas kernels  59.9 us (100%)
    pallas_call x1, Pallas kernels, local_product(): pl.pallas_call(functools.partial(kernel, n_x, n_y), out_shape=(pltpu.VMEM...  57.7 us
    pallas_call x1, Pallas kernels, local_product(): pl.pallas_call(functools.partial(finish, n_x), out_shape=pltpu.HBM((rows,...  2.17 us

profile of v19, /device:TPU:0, one launch (start us, length us, event | category | flops | bytes accessed | tf_op | source)
XLA Modules:
  0.0 59.9 jit_solution(6732637651425342241)
XLA Ops:
  0.0 57.7 %gather_dot.1 = (f32[1536,768]{1,0:T(8,128)S(1)}, bf16[1536,1536]{1,0:T(8,128)(2,1)S(1)}, bf16[2,1536,768]{2,1,0:T(8,128)(2,1)S(1)}) custom-call(bf16[1536,1536]{1,0:T(8,128)(2,1)} %a_hbm.1, bf16[1536,1536]{1,0:T(8,128)(2,1)} %b_hbm.1), custom_call_target="tpu_custom_call" | custom-call | tf_op jit(solution)/shard_map/gather_dot/pallas_call | solution.py:204
  57.7 2.2 %finish.1 = f32[1536,768]{1,0:T(8,128)} custom-call(f32[1536,768]{1,0:T(8,128)S(1)} %get-tuple-element.8.c_ref, bf16[1536,1536]{1,0:T(8,128)(2,1)S(1)} %get-tuple-element.9.a_rem, bf16[2,1536,768]{2,1,0:T(8,128)(2,1)S(1)} %get-tuple-element.10.b_full), custom_call_target="tpu_custom_call" | custom-call | tf_op jit(solution)/shard_map/finish/pallas_call | solution.py:230

commit v20 on v19

--- a/solution.py
+++ b/solution.py
@@ -15,7 +15,7 @@
 HEAD = 64 // CHUNK
 NEXT = 256 // CHUNK
 BLOCK = 256
-HOLD = 21
+HOLD = 19
 WARM = 96 // CHUNK
 
 

time: 60 us -> 60 us (level)
  no operation moved by 1% of the time
where the time goes in v20:
time: 60 us; the launch traced here: 59.9 us
  Pallas kernels  59.9 us (100%)
    pallas_call x1, Pallas kernels, local_product(): pl.pallas_call(functools.partial(kernel, n_x, n_y), out_shape=(pltpu.VMEM...  57.7 us
    pallas_call x1, Pallas kernels, local_product(): pl.pallas_call(functools.partial(finish, n_x), out_shape=pltpu.HBM((rows,...  2.17 us

profile of v20, /device:TPU:0, one launch (start us, length us, event | category | flops | bytes accessed | tf_op | source)
XLA Modules:
  0.0 59.9 jit_solution(14311688227120114477)
XLA Ops:
  0.0 57.7 %gather_dot.1 = (f32[1536,768]{1,0:T(8,128)S(1)}, bf16[1536,1536]{1,0:T(8,128)(2,1)S(1)}, bf16[2,1536,768]{2,1,0:T(8,128)(2,1)S(1)}) custom-call(bf16[1536,1536]{1,0:T(8,128)(2,1)} %a_hbm.1, bf16[1536,1536]{1,0:T(8,128)(2,1)} %b_hbm.1), custom_call_target="tpu_custom_call" | custom-call | tf_op jit(solution)/shard_map/gather_dot/pallas_call | solution.py:204
  57.7 2.2 %finish.1 = f32[1536,768]{1,0:T(8,128)} custom-call(f32[1536,768]{1,0:T(8,128)S(1)} %get-tuple-element.8.c_ref, bf16[1536,1536]{1,0:T(8,128)(2,1)S(1)} %get-tuple-element.9.a_rem, bf16[2,1536,768]{2,1,0:T(8,128)(2,1)S(1)} %get-tuple-element.10.b_full), custom_call_target="tpu_custom_call" | custom-call | tf_op jit(solution)/shard_map/finish/pallas_call | solution.py:230
